TPU v7x, 512 devices: a whole 4x8x8 slice. The times are simulated.
512 devices in a mesh: tok: 8 (over x, core), voc: 64 (over z, y).
Axes of the slice: x: 4, y: 8, z: 8, core: 2. Of those that a mesh axis runs over, the one named last changes fastest.
Arguments:
- hidden: bfloat16 [1024, 4608], P(('tok', 'voc')), may hold values from -6 to 6
- norm_gain: float32 [4608], replicated, may hold values from 0.25 to 1.75
- head_weight: bfloat16 [262144, 4608], P(('tok', 'voc')), may hold values from -0.26367188 to 0.26367188
- targets: int32 [1024], replicated, may hold values from 0 to 262143
- lengths: int32 [32], replicated, may hold values from 1 to 32
Outputs:
- token_loss: float32 [1024], P(('tok', 'voc'))
- mean_loss: float32 [], replicated
All inputs are finite; a program needn't handle non-finite values.
Results may differ from a plain program's by a relative error of at most 0.00051.
Values may be sent and summed in bfloat16 or wider, within the bound.
No kernel may reach another device: no remote copies, remote signals or barrier semaphores. Data moves between devices by JAX's collectives and lax.ppermute only.
A program may use at most 64 MiB of HBM per device.

v0:
```python
import jax
import jax.numpy as jnp
from jax import lax
from jax.experimental import pallas as pl
from jax.experimental.pallas import tpu as pltpu
from jax.sharding import Mesh
from jax.sharding import PartitionSpec as P

WINDOW = 32
TOK_VOC = ("x", "c", "z", "y")
PLANE = ("z", "y")
WIDE = 3584
TILE = 512
STRIP = 64
VMEM_LIMIT = 46 * 2**20


def params(serial=False):
    order = {"dimension_semantics": ("arbitrary",)} if serial else {}
    return pltpu.CompilerParams(vmem_limit_bytes=VMEM_LIMIT, **order)


def whole(shape):
    return pl.BlockSpec(shape, lambda *_: (0,) * len(shape))


def scalars():
    return pl.BlockSpec(memory_space=pltpu.SMEM)


def dot_t(a, b):
    return lax.dot_general(a, b, (((1,), (1,)), ((), ())), preferred_element_type=jnp.float32)


def norm_kernel(hidden, gain, wide, narrow):
    values = hidden[...].astype(jnp.float32)
    meansq = jnp.mean(values * values, axis=1, keepdims=True)
    normed = (values * lax.rsqrt(meansq + 1e-06) * gain[...]).astype(jnp.bfloat16)
    width = wide.shape[2]
    narrow[...] = normed[:, width:]
    for i in range(wide.shape[0]):
        wide[i] = normed[:, :width]


def norm(hidden, gain, copies, width):
    rows, depth = hidden.shape
    shapes = [(copies, rows, width), (rows, depth - width)]
    return pl.pallas_call(
        norm_kernel,
        in_specs=[whole(hidden.shape), whole((1, depth))],
        out_specs=[whole(s) for s in shapes],
        out_shape=[jax.ShapeDtypeStruct(s, jnp.bfloat16) for s in shapes],
        compiler_params=params(),
        name="norm",
    )(hidden, gain.reshape(1, depth))


def first_kernel(wide_steps, *refs):
    xs, (mixed, w0, w1, out) = refs[:-4], refs[-4:]
    step = pl.program_id(0)
    weight = jnp.concatenate([w0[...], w1[...]], axis=0)
    early = sum(x.shape[0] for x in xs)

    @pl.when(step < wide_steps)
    def _():
        part = dot_t(weight, jnp.concatenate([x[...] for x in xs], axis=0))

        @pl.when(step == 0)
        def _():
            out[:, :early] = part

        @pl.when(step > 0)
        def _():
            out[:, :early] += part

    @pl.when(step >= wide_steps)
    def _():
        tokens = mixed.shape[0]
        groups = tokens // 128
        row = lax.broadcasted_iota(jnp.int32, (tokens, tokens), 0)
        col = lax.broadcasted_iota(jnp.int32, (tokens, tokens), 1)
        inner = row & 127
        pick = (inner >> 1) * (2 * groups) + (row >> 7) * 2 + (inner & 1)
        chosen = jnp.where(col == pick, 1.0, 0.0).astype(jnp.bfloat16)
        rows = jnp.dot(chosen, mixed[...], preferred_element_type=jnp.float32).astype(jnp.bfloat16)
        part = dot_t(weight, rows)
        out[:, :early] += part[:, :early]

        @pl.when(step == wide_steps)
        def _():
            out[:, early:] = part[:, early:]

        @pl.when(step > wide_steps)
        def _():
            out[:, early:] += part[:, early:]


def first_product(xs, mixed, w0, w1):
    vocab, depth = w0.shape
    wide_steps = xs[0].shape[1] // TILE
    steps = depth // TILE
    tokens = mixed.shape[0]
    return pl.pallas_call(
        lambda *refs: first_kernel(wide_steps, *refs),
        grid=(steps,),
        in_specs=[pl.BlockSpec((x.shape[0], TILE), lambda k: (0, jnp.minimum(k, wide_steps - 1))) for x in xs]
        + [pl.BlockSpec((tokens, TILE), lambda k: (0, jnp.maximum(k - wide_steps, 0)))]
        + [pl.BlockSpec((vocab, TILE), lambda k: (0, k))] * 2,
        out_specs=whole((2 * vocab, tokens)),
        out_shape=jax.ShapeDtypeStruct((2 * vocab, tokens), jnp.float32),
        compiler_params=params(serial=True),
        cost_estimate=pl.CostEstimate(flops=2 * vocab * tokens * depth, bytes_accessed=14 * 2**20, transcendentals=0),
        name="first_product",
    )(*xs, mixed, w0, w1)


def second_kernel(place, targets, near, *refs):
    xs, (w0, w1, out, late, stat) = refs[:-5], refs[-5:]
    step = pl.program_id(0)
    vocab = w0.shape[0]
    early = near.shape[1] - late.shape[1]
    tokens = near.shape[1]
    groups = tokens // 128
    weight = jnp.concatenate([w0[...], w1[...]], axis=0)
    part = dot_t(weight, jnp.concatenate([x[...] for x in xs], axis=0))

    @pl.when(step == 0)
    def _():
        late[...] = near[:, early:] + part

    @pl.when(step > 0)
    def _():
        late[...] += part

    @pl.when(step == pl.num_programs(0) - 1)
    def _():
        wanted = jnp.concatenate([targets[pl.ds(place[3 + k] * 2 + place[0], 1), :] for k in range(groups)], axis=1)
        expsum = jnp.zeros((8, tokens), jnp.float32)
        picked = jnp.zeros((8, tokens), jnp.float32)
        for r in range(0, 2 * vocab, STRIP):
            logits = jnp.concatenate([near[r:r + STRIP, :early], late[r:r + STRIP, :]], axis=1)
            capped = 30.0 * jnp.tanh(logits / 30.0)
            local = wanted - (place[1 + r // vocab] + r % vocab)
            column = lax.broadcasted_iota(jnp.int32, (STRIP, tokens), 0)
            hit = jnp.where(column == local, capped, 0.0)
            expsum += jnp.sum(jnp.exp(capped).reshape(STRIP // 8, 8, tokens), axis=0)
            picked += jnp.sum(hit.reshape(STRIP // 8, 8, tokens), axis=0)
        for i, total in enumerate((expsum, picked)):
            total = jnp.sum(total, axis=0, keepdims=True)
            for k in range(groups):
                stat[pl.ds(place[3 + k] + i * groups, 1), :] = total[:, k * 128:(k + 1) * 128]
        for i in range(out.shape[0]):
            out[i] = stat[...]


def second_product(place, targets, near, xs, w0, w1, copies):
    vocab, _ = w0.shape
    wide = xs[0].shape[1]
    tokens = near.shape[1]
    late = sum(x.shape[0] for x in xs)
    rows = 2 * tokens // 128
    return pl.pallas_call(
        second_kernel,
        grid=(wide // TILE,),
        in_specs=[scalars(), whole(targets.shape), whole(near.shape)]
        + [pl.BlockSpec((x.shape[0], TILE), lambda k: (0, k)) for x in xs]
        + [pl.BlockSpec((vocab, TILE), lambda k: (0, k))] * 2,
        out_specs=whole((copies, rows, 128)),
        out_shape=jax.ShapeDtypeStruct((copies, rows, 128), jnp.float32),
        scratch_shapes=[pltpu.VMEM((2 * vocab, late), jnp.float32), pltpu.VMEM((rows, 128), jnp.float32)],
        compiler_params=params(serial=True),
        cost_estimate=pl.CostEstimate(flops=4 * vocab * late * wide, bytes_accessed=10 * 2**20, transcendentals=0),
        name="second_product",
    )(place, targets, near, *xs, w0, w1)


def join_kernel(parts, out):
    total = jnp.sum(parts[...], axis=0)
    for i in range(out.shape[0]):
        out[i] = total


def join(parts, copies):
    shape = (copies, *parts.shape[1:])
    return pl.pallas_call(
        join_kernel,
        in_specs=[whole(parts.shape)],
        out_specs=whole(shape),
        out_shape=jax.ShapeDtypeStruct(shape, jnp.float32),
        compiler_params=params(),
        name="join",
    )(parts)


def loss_kernel(place, count, live, parts, token_loss, mean_loss, loss):
    groups = parts.shape[1] // 2
    for core in range(2):
        total = parts[core]
        for i in range(core + 2, parts.shape[0], 2):
            total = total + parts[i]
        rows = slice(core * groups, (core + 1) * groups)
        loss[rows, :] = live[rows, :] * (jnp.log(total[:groups]) - total[groups:])
    mean_loss[0] = jnp.sum(loss[...]) / count[0]
    own = loss[pl.ds(place[0], 1), :]
    lane = lax.broadcasted_iota(jnp.int32, own.shape, 1)
    for i in range(token_loss.shape[0]):
        token_loss[i] = jnp.sum(jnp.where(lane == place[1] + i, own, 0.0))


def final_loss(place, count, live, parts, own_rows):
    return pl.pallas_call(
        loss_kernel,
        in_specs=[scalars(), scalars(), whole(live.shape), whole(parts.shape)],
        out_specs=[scalars(), scalars()],
        out_shape=[jax.ShapeDtypeStruct((own_rows,), jnp.float32), jax.ShapeDtypeStruct((1,), jnp.float32)],
        scratch_shapes=[pltpu.VMEM(live.shape, jnp.float32)],
        compiler_params=params(),
        name="final_loss",
    )(place, count, live, parts)


def exchange(value, axes):
    return lax.all_to_all(value, axes, 0, 0)


def body(hidden, norm_gain, head_weight, targets, lengths):
    own_rows = hidden.shape[0]
    vocab_rows = head_weight.shape[0]
    nx, nc = lax.axis_size("x"), lax.axis_size("c")
    plane = lax.axis_size(PLANE)
    x, c = lax.axis_index("x"), lax.axis_index("c")
    seat = lax.axis_index(PLANE)
    block = plane * own_rows

    def turn(value, k):
        return lax.ppermute(value, "x", [(i, (i + k) % nx) for i in range(nx)])

    wide, narrow = norm(hidden, norm_gain, plane, WIDE)
    mine = exchange(wide, PLANE).reshape(block, WIDE)
    other_weight = lax.ppermute(head_weight, "c", [(0, 1), (1, 0)])
    column = jnp.concatenate([narrow, turn(narrow, 1), turn(narrow, nx - 1), turn(narrow, 2)], axis=0)
    mixed = exchange(jnp.broadcast_to(column[None], (plane, *column.shape)), PLANE).reshape(nx * block, -1)
    low, high = mine[:block // 2], mine[block // 2:]
    up_low, down_high = turn(low, 1), turn(high, nx - 1)
    up_high, down_low = turn(high, 1), turn(low, nx - 1)
    far_low, far_high = turn(up_low, 1), turn(down_high, nx - 1)
    near = first_product((low, high, up_low, up_high), mixed, head_weight, other_weight)
    sources = [lax.rem(x + nx - k, nx) for k in (0, 1, nx - 1, 2)]
    first = ((x * nc + c) * plane + seat) * vocab_rows
    second = ((x * nc + 1 - c) * plane + seat) * vocab_rows
    place = jnp.stack([c, first, second, *sources]).astype(jnp.int32)
    stats = second_product(
        place, targets.reshape(nx * nc, block), near, (down_low, down_high, far_low, far_high),
        head_weight, other_weight, plane,
    )
    stats = join(exchange(stats, PLANE), nx * nc)
    stats = exchange(stats, ("x", "c"))
    position = jnp.arange(WINDOW, dtype=jnp.int32)
    live = (position[None, :] < lengths[:, None]).astype(jnp.float32).reshape(nx, nc, block)
    live = live.transpose(1, 0, 2).reshape(nx * nc, block)
    count = jnp.sum(lengths.astype(jnp.float32)).reshape(1)
    seat_of = jnp.stack([c * nx + x, seat * own_rows]).astype(jnp.int32)
    token_loss, mean_loss = final_loss(seat_of, count, live, stats, own_rows)
    return (token_loss, mean_loss.reshape(()))


def solution(mesh):
    split = Mesh(mesh.devices.reshape(4, 2, 8, 8), TOK_VOC)
    in_specs = (P(TOK_VOC, None), P(), P(TOK_VOC, None), P(), P())
    out_specs = (P(TOK_VOC), P())
    return jax.shard_map(body, mesh=split, in_specs=in_specs, out_specs=out_specs, check_vma=False)
```

profile of v0, /device:TPU:1, one launch (start us, length us, event | category | flops | bytes accessed | tf_op | source)
XLA Modules:
  0.0 142.5 jit_solution(17869334634089581131)
XLA Ops:
  0.6 8.8 %collective-permute-start.5 = (bf16[512,4608]{1,0:T(8,128)(2,1)}, bf16[512,4608]{1,0:T(8,128)(2,1)}, u32[]{:S(2)}, u32[]{:S(2)}) collective-permute-start(bf16[512,4608]{1,0:T(8,128)(2,1)} %refs_4_.1), channel_id=1, source_target_pairs={{0,64},{64,0},{1,65},{65,1},{2,66},{66,2},{3,67},{67,3},{4,68},{68... | collective-permute-start | bytes 14155784 | tf_op jit(solution)/shard_map/ppermute | solution.py:240
  9.4 0.7 reshape.38.gain
  10.1 0.0 copy-start
  10.1 0.7 copy-done
  10.9 1.2 norm.1
  12.0 11.0 %all-to-all-start = ((bf16[64,2,3584]{2,1,0:T(2,128)(2,1)}), bf16[64,2,3584]{2,1,0:T(2,128)(2,1)S(1)}, u32[]{:S(2)}, u32[]{:S(2)}) async-start(bf16[64,2,3584]{2,1,0:T(2,128)(2,1)} %get-tuple-element.6), calls=%async_computation | async-start | bytes 1835008 | tf_op jit(solution)/shard_map/all_to_all | solution.py:223
  23.0 3.1 %collective-permute-start.2 = (bf16[2,1024]{1,0:T(2,128)(2,1)S(1)}, bf16[2,1024]{1,0:T(2,128)(2,1)S(1)}, u32[]{:S(2)}, u32[]{:S(2)}) collective-permute-start(bf16[2,1024]{1,0:T(2,128)(2,1)S(1)} %get-tuple-element.7), channel_id=1, source_target_pairs={{0,128},{128,256},{256,384},{384,0},{1,129},{129,257},{257,385},{3... | collective-permute-start | bytes 12296 | tf_op jit(solution)/shard_map/ppermute | solution.py:236
  26.1 3.4 %collective-permute-start.3 = (bf16[2,1024]{1,0:T(2,128)(2,1)S(1)}, bf16[2,1024]{1,0:T(2,128)(2,1)S(1)}, u32[]{:S(2)}, u32[]{:S(2)}) collective-permute-start(bf16[2,1024]{1,0:T(2,128)(2,1)S(1)} %get-tuple-element.7), channel_id=1, source_target_pairs={{0,384},{128,0},{256,128},{384,256},{1,385},{129,1},{257,129},{385... | collective-permute-start | bytes 12296 | tf_op jit(solution)/shard_map/ppermute | solution.py:236
  29.5 3.4 %collective-permute-start.4 = (bf16[2,1024]{1,0:T(2,128)(2,1)S(1)}, bf16[2,1024]{1,0:T(2,128)(2,1)S(1)}, u32[]{:S(2)}, u32[]{:S(2)}) collective-permute-start(bf16[2,1024]{1,0:T(2,128)(2,1)S(1)} %get-tuple-element.7), channel_id=1, source_target_pairs={{0,256},{128,384},{256,0},{384,128},{1,257},{129,385},{257,1},{385... | collective-permute-start | bytes 12296 | tf_op jit(solution)/shard_map/ppermute | solution.py:236
  32.9 0.0 collective-permute-done.2
  33.0 0.0 collective-permute-done.3
  33.0 2.7 %collective-permute-done.4 = bf16[2,1024]{1,0:T(2,128)(2,1)S(1)} collective-permute-done((bf16[2,1024]{1,0:T(2,128)(2,1)S(1)}, bf16[2,1024]{1,0:T(2,128)(2,1)S(1)}, u32[]{:S(2)}, u32[]{:S(2)}) %collective-permute-start.4) | collective-permute-done | bytes 4128 | tf_op jit(solution)/shard_map/ppermute | solution.py:236
  35.7 12.7 %all-to-all-done = bf16[64,2,3584]{2,1,0:T(2,128)(2,1)S(1)} async-done(((bf16[64,2,3584]{2,1,0:T(2,128)(2,1)}), bf16[64,2,3584]{2,1,0:T(2,128)(2,1)S(1)}, u32[]{:S(2)}, u32[]{:S(2)}) %all-to-all-start) | async-done | bytes 917536 | tf_op jit(solution)/shard_map/all_to_all | solution.py:223
  48.4 1.1 broadcast_in_dim.2
  49.5 7.5 %all-to-all-start.1 = ((bf16[64,8,1024]{2,1,0:T(8,128)(2,1)}), bf16[64,8,1024]{2,1,0:T(8,128)(2,1)S(1)}, u32[]{:S(2)}, u32[]{:S(2)}) async-start(bf16[64,8,1024]{2,1,0:T(8,128)(2,1)} %broadcast_in_dim.2), calls=%async_computation.1 | async-start | bytes 2097152 | tf_op jit(solution)/shard_map/all_to_all | solution.py:223
  57.1 0.6 fusion
  57.7 0.2 slice.13.refs_0_
  57.9 3.1 %collective-permute-start = (bf16[64,3584]{1,0:T(8,128)(2,1)S(1)}, bf16[64,3584]{1,0:T(8,128)(2,1)S(1)}, u32[]{:S(2)}, u32[]{:S(2)}) collective-permute-start(bf16[64,3584]{1,0:T(8,128)(2,1)S(1)} %slice.13.refs_0_), channel_id=1, source_target_pairs={{0,128},{128,256},{256,384},{384,0},{1,129},{129,257},{257,385},{3... | collective-permute-start | bytes 1376264 | tf_op jit(solution)/shard_map/ppermute | solution.py:236
  61.0 0.2 slice.15.refs_1_
  61.2 3.4 %collective-permute-start.7 = (bf16[64,3584]{1,0:T(8,128)(2,1)S(1)}, bf16[64,3584]{1,0:T(8,128)(2,1)S(1)}, u32[]{:S(2)}, u32[]{:S(2)}) collective-permute-start(bf16[64,3584]{1,0:T(8,128)(2,1)S(1)} %slice.15.refs_1_), channel_id=1, source_target_pairs={{0,384},{128,0},{256,128},{384,256},{1,385},{129,1},{257,129},{385... | collective-permute-start | bytes 1376264 | tf_op jit(solution)/shard_map/ppermute | solution.py:236
  64.6 1.9 %collective-permute-start.1 = (bf16[64,3584]{1,0:T(8,128)(2,1)S(1)}, bf16[64,3584]{1,0:T(8,128)(2,1)S(1)}, u32[]{:S(2)}, u32[]{:S(2)}) collective-permute-start(bf16[64,3584]{1,0:T(8,128)(2,1)S(1)} %slice.15.refs_1_), channel_id=1, source_target_pairs={{0,128},{128,256},{256,384},{384,0},{1,129},{129,257},{257,385},{3... | collective-permute-start | bytes 1376264 | tf_op jit(solution)/shard_map/ppermute | solution.py:236
  66.5 4.6 %collective-permute-start.6 = (bf16[64,3584]{1,0:T(8,128)(2,1)S(1)}, bf16[64,3584]{1,0:T(8,128)(2,1)}, u32[]{:S(2)}, u32[]{:S(2)}) collective-permute-start(bf16[64,3584]{1,0:T(8,128)(2,1)S(1)} %slice.13.refs_0_), channel_id=1, source_target_pairs={{0,384},{128,0},{256,128},{384,256},{1,385},{129,1},{257,129},{385... | collective-permute-start | bytes 1376264 | tf_op jit(solution)/shard_map/ppermute | solution.py:236
  71.1 0.5 collective-permute-done.refs_2_
  71.6 1.9 %collective-permute-start.8 = (bf16[64,3584]{1,0:T(8,128)(2,1)S(1)}, bf16[64,3584]{1,0:T(8,128)(2,1)}, u32[]{:S(2)}, u32[]{:S(2)}) collective-permute-start(bf16[64,3584]{1,0:T(8,128)(2,1)S(1)} %collective-permute-done.refs_2_), channel_id=1, source_target_pairs={{0,128},{128,256},{256,384},{384,0},{1,129},{129,257},{257,385},{3... | collective-permute-start | bytes 1376264 | tf_op jit(solution)/shard_map/ppermute | solution.py:236
  73.5 0.0 collective-permute-done.7.refs_1_
  73.5 4.6 %collective-permute-start.9 = (bf16[64,3584]{1,0:T(8,128)(2,1)S(1)}, bf16[64,3584]{1,0:T(8,128)(2,1)}, u32[]{:S(2)}, u32[]{:S(2)}) collective-permute-start(bf16[64,3584]{1,0:T(8,128)(2,1)S(1)} %collective-permute-done.7.refs_1_), channel_id=1, source_target_pairs={{0,384},{128,0},{256,128},{384,256},{1,385},{129,1},{257,129},{385... | collective-permute-start | bytes 1376264 | tf_op jit(solution)/shard_map/ppermute | solution.py:236
  78.1 0.1 stack.43.place
  78.2 5.7 %all-to-all-done.1 = bf16[64,8,1024]{2,1,0:T(8,128)(2,1)S(1)} async-done(((bf16[64,8,1024]{2,1,0:T(8,128)(2,1)}), bf16[64,8,1024]{2,1,0:T(8,128)(2,1)S(1)}, u32[]{:S(2)}, u32[]{:S(2)}) %all-to-all-start.1) | async-done | bytes 1048608 | tf_op jit(solution)/shard_map/all_to_all | solution.py:223
  83.9 0.0 collective-permute-done.1.refs_3_
  83.9 0.0 collective-permute-done.5.refs_6_.refs_5_
  83.9 10.6 %first_product.1.near = f32[1024,512]{1,0:T(8,128)S(1)} custom-call(bf16[64,3584]{1,0:T(8,128)(2,1)S(1)} %slice.13.refs_0_, bf16[64,3584]{1,0:T(8,128)(2,1)S(1)} %slice.15.refs_1_, bf16[64,3584]{1,0:T(8,128)(2,1)S(1)} %collective-permute-done.refs_2_, bf16[64,3584]{1,0:T(8,128)(2,1)S(1)} %collective-permute-done.1.refs_3_, bf16[512,1024]{1,0:T(8,128)(2,1)S(1)} %bitcast.18, ...), custom_call_target="tpu_custom_call" | custom-call | flops 2415919104 | bytes 14680064 | tf_op jit(solution)/shard_map/first_product/pallas_call | solution.py:103
  94.5 0.0 collective-permute-done.6.refs_0_
  94.6 0.0 collective-permute-done.8.refs_2_
  94.6 0.0 collective-permute-done.9.refs_3_
  94.6 0.0 copy-start.2
  94.6 9.2 %second_product.1 = f32[64,8,128]{2,1,0:T(8,128)} custom-call(s32[7]{0:T(128)S(1)} %stack.43.place, s32[8,128]{1,0:T(8,128)S(1)} %bitcast.20, f32[1024,512]{1,0:T(8,128)S(1)} %first_product.1.near, bf16[64,3584]{1,0:T(8,128)(2,1)} %collective-permute-done.6.refs_0_, bf16[64,3584]{1,0:T(8,128)(2,1)S(1)} %collective-permute-done.7.refs_1_, ...), custom_call_target="tpu_custom_call" | custom-call | flops 1879048192 | bytes 10485760 | tf_op jit(solution)/shard_map/second_product/pallas_call | solution.py:162
  103.8 10.4 %all-to-all-start.2 = ((f32[64,8,128]{2,1,0:T(8,128)}), f32[64,8,128]{2,1,0:T(8,128)S(1)}, u32[]{:S(2)}, u32[]{:S(2)}) async-start(f32[64,8,128]{2,1,0:T(8,128)} %second_product.1), calls=%async_computation.2 | async-start | bytes 524288 | tf_op jit(solution)/shard_map/all_to_all | solution.py:223
  114.2 0.1 lt.25
  114.3 0.1 lt.26
  114.4 0.1 lt.27
  114.5 0.1 lt.23
  114.5 0.7 convert_reduce_fusion
  115.2 11.5 %all-to-all-done.2.parts = f32[64,8,128]{2,1,0:T(8,128)S(1)} async-done(((f32[64,8,128]{2,1,0:T(8,128)}), f32[64,8,128]{2,1,0:T(8,128)S(1)}, u32[]{:S(2)}, u32[]{:S(2)}) %all-to-all-start.2) | async-done | bytes 262176 | tf_op jit(solution)/shard_map/all_to_all | solution.py:223
  126.7 0.7 join.1
  127.4 8.5 %all-to-all-start.3 = ((f32[8,8,128]{2,1,0:T(8,128)}), f32[8,8,128]{2,1,0:T(8,128)S(1)}, u32[]{:S(2)}, u32[]{:S(2)}) async-start(f32[8,8,128]{2,1,0:T(8,128)} %join.1), calls=%async_computation.3 | async-start | bytes 65536 | tf_op jit(solution)/shard_map/all_to_all | solution.py:223
  135.9 0.1 pad_add_fusion.place
  136.0 4.6 %all-to-all-done.3.parts = f32[8,8,128]{2,1,0:T(8,128)S(1)} async-done(((f32[8,8,128]{2,1,0:T(8,128)}), f32[8,8,128]{2,1,0:T(8,128)S(1)}, u32[]{:S(2)}, u32[]{:S(2)}) %all-to-all-start.3) | async-done | bytes 32800 | tf_op jit(solution)/shard_map/all_to_all | solution.py:223
  140.6 1.8 %final_loss.1 = (f32[2]{0:T(128)}, f32[1]{0:T(128)}) custom-call(s32[2]{0:T(128)S(1)} %pad_add_fusion.place, f32[1]{0:T(128)} %bitcast.2.count, f32[8,128]{1,0:T(8,128)S(1)} %bitcast.19, f32[8,8,128]{2,1,0:T(8,128)S(1)} %all-to-all-done.3.parts), custom_call_target="tpu_custom_call" | custom-call | tf_op jit(solution)/shard_map/final_loss/pallas_call | solution.py:211
  (7 shorter events, 0.0 us)
Async XLA Ops:
  0.6 83.3 %collective-permute-start.5 = (bf16[512,4608]{1,0:T(8,128)(2,1)}, bf16[512,4608]{1,0:T(8,128)(2,1)}, u32[]{:S(2)}, u32[]{:S(2)}) collective-permute-start(bf16[512,4608]{1,0:T(8,128)(2,1)} %refs_4_.1), channel_id=1, source_target_pairs={{0,64},{64,0},{1,65},{65,1},{2,66},{66,2},{3,67},{67,3},{4,68},{68... | collective-permute-start | bytes 14155784 | tf_op jit(solution)/shard_map/ppermute | solution.py:240
  10.1 0.7 copy-start
  12.0 36.4 %all-to-all-start = ((bf16[64,2,3584]{2,1,0:T(2,128)(2,1)}), bf16[64,2,3584]{2,1,0:T(2,128)(2,1)S(1)}, u32[]{:S(2)}, u32[]{:S(2)}) async-start(bf16[64,2,3584]{2,1,0:T(2,128)(2,1)} %get-tuple-element.6), calls=%async_computation | async-start | bytes 1835008 | tf_op jit(solution)/shard_map/all_to_all | solution.py:223
  23.0 10.0 %collective-permute-start.2 = (bf16[2,1024]{1,0:T(2,128)(2,1)S(1)}, bf16[2,1024]{1,0:T(2,128)(2,1)S(1)}, u32[]{:S(2)}, u32[]{:S(2)}) collective-permute-start(bf16[2,1024]{1,0:T(2,128)(2,1)S(1)} %get-tuple-element.7), channel_id=1, source_target_pairs={{0,128},{128,256},{256,384},{384,0},{1,129},{129,257},{257,385},{3... | collective-permute-start | bytes 12296 | tf_op jit(solution)/shard_map/ppermute | solution.py:236
  26.1 6.8 %collective-permute-start.3 = (bf16[2,1024]{1,0:T(2,128)(2,1)S(1)}, bf16[2,1024]{1,0:T(2,128)(2,1)S(1)}, u32[]{:S(2)}, u32[]{:S(2)}) collective-permute-start(bf16[2,1024]{1,0:T(2,128)(2,1)S(1)} %get-tuple-element.7), channel_id=1, source_target_pairs={{0,384},{128,0},{256,128},{384,256},{1,385},{129,1},{257,129},{385... | collective-permute-start | bytes 12296 | tf_op jit(solution)/shard_map/ppermute | solution.py:236
  29.5 6.2 %collective-permute-start.4 = (bf16[2,1024]{1,0:T(2,128)(2,1)S(1)}, bf16[2,1024]{1,0:T(2,128)(2,1)S(1)}, u32[]{:S(2)}, u32[]{:S(2)}) collective-permute-start(bf16[2,1024]{1,0:T(2,128)(2,1)S(1)} %get-tuple-element.7), channel_id=1, source_target_pairs={{0,256},{128,384},{256,0},{384,128},{1,257},{129,385},{257,1},{385... | collective-permute-start | bytes 12296 | tf_op jit(solution)/shard_map/ppermute | solution.py:236
  49.5 34.4 %all-to-all-start.1 = ((bf16[64,8,1024]{2,1,0:T(8,128)(2,1)}), bf16[64,8,1024]{2,1,0:T(8,128)(2,1)S(1)}, u32[]{:S(2)}, u32[]{:S(2)}) async-start(bf16[64,8,1024]{2,1,0:T(8,128)(2,1)} %broadcast_in_dim.2), calls=%async_computation.1 | async-start | bytes 2097152 | tf_op jit(solution)/shard_map/all_to_all | solution.py:223
  57.9 13.7 %collective-permute-start = (bf16[64,3584]{1,0:T(8,128)(2,1)S(1)}, bf16[64,3584]{1,0:T(8,128)(2,1)S(1)}, u32[]{:S(2)}, u32[]{:S(2)}) collective-permute-start(bf16[64,3584]{1,0:T(8,128)(2,1)S(1)} %slice.13.refs_0_), channel_id=1, source_target_pairs={{0,128},{128,256},{256,384},{384,0},{1,129},{129,257},{257,385},{3... | collective-permute-start | bytes 1376264 | tf_op jit(solution)/shard_map/ppermute | solution.py:236
  61.2 12.3 %collective-permute-start.7 = (bf16[64,3584]{1,0:T(8,128)(2,1)S(1)}, bf16[64,3584]{1,0:T(8,128)(2,1)S(1)}, u32[]{:S(2)}, u32[]{:S(2)}) collective-permute-start(bf16[64,3584]{1,0:T(8,128)(2,1)S(1)} %slice.15.refs_1_), channel_id=1, source_target_pairs={{0,384},{128,0},{256,128},{384,256},{1,385},{129,1},{257,129},{385... | collective-permute-start | bytes 1376264 | tf_op jit(solution)/shard_map/ppermute | solution.py:236
  64.6 19.3 %collective-permute-start.1 = (bf16[64,3584]{1,0:T(8,128)(2,1)S(1)}, bf16[64,3584]{1,0:T(8,128)(2,1)S(1)}, u32[]{:S(2)}, u32[]{:S(2)}) collective-permute-start(bf16[64,3584]{1,0:T(8,128)(2,1)S(1)} %slice.15.refs_1_), channel_id=1, source_target_pairs={{0,128},{128,256},{256,384},{384,0},{1,129},{129,257},{257,385},{3... | collective-permute-start | bytes 1376264 | tf_op jit(solution)/shard_map/ppermute | solution.py:236
  66.5 28.0 %collective-permute-start.6 = (bf16[64,3584]{1,0:T(8,128)(2,1)S(1)}, bf16[64,3584]{1,0:T(8,128)(2,1)}, u32[]{:S(2)}, u32[]{:S(2)}) collective-permute-start(bf16[64,3584]{1,0:T(8,128)(2,1)S(1)} %slice.13.refs_0_), channel_id=1, source_target_pairs={{0,384},{128,0},{256,128},{384,256},{1,385},{129,1},{257,129},{385... | collective-permute-start | bytes 1376264 | tf_op jit(solution)/shard_map/ppermute | solution.py:236
  71.6 23.0 %collective-permute-start.8 = (bf16[64,3584]{1,0:T(8,128)(2,1)S(1)}, bf16[64,3584]{1,0:T(8,128)(2,1)}, u32[]{:S(2)}, u32[]{:S(2)}) collective-permute-start(bf16[64,3584]{1,0:T(8,128)(2,1)S(1)} %collective-permute-done.refs_2_), channel_id=1, source_target_pairs={{0,128},{128,256},{256,384},{384,0},{1,129},{129,257},{257,385},{3... | collective-permute-start | bytes 1376264 | tf_op jit(solution)/shard_map/ppermute | solution.py:236
  73.5 21.0 %collective-permute-start.9 = (bf16[64,3584]{1,0:T(8,128)(2,1)S(1)}, bf16[64,3584]{1,0:T(8,128)(2,1)}, u32[]{:S(2)}, u32[]{:S(2)}) collective-permute-start(bf16[64,3584]{1,0:T(8,128)(2,1)S(1)} %collective-permute-done.7.refs_1_), channel_id=1, source_target_pairs={{0,384},{128,0},{256,128},{384,256},{1,385},{129,1},{257,129},{385... | collective-permute-start | bytes 1376264 | tf_op jit(solution)/shard_map/ppermute | solution.py:236
  83.9 10.7 %copy-start.1 = (s32[1024]{0:T(1024)S(1)}, s32[1024]{0:T(1024)}, u32[]{:S(2)}) copy-start(s32[1024]{0:T(1024)} %param.8) | copy-start | bytes 12292
  94.6 19.6 %copy-start.2 = (s32[32]{0:T(128)S(1)}, s32[32]{0:T(128)}, u32[]{:S(2)}) copy-start(s32[32]{0:T(128)} %param.9) | copy-start | bytes 388
  103.8 22.9 %all-to-all-start.2 = ((f32[64,8,128]{2,1,0:T(8,128)}), f32[64,8,128]{2,1,0:T(8,128)S(1)}, u32[]{:S(2)}, u32[]{:S(2)}) async-start(f32[64,8,128]{2,1,0:T(8,128)} %second_product.1), calls=%async_computation.2 | async-start | bytes 524288 | tf_op jit(solution)/shard_map/all_to_all | solution.py:223
  127.4 13.3 %all-to-all-start.3 = ((f32[8,8,128]{2,1,0:T(8,128)}), f32[8,8,128]{2,1,0:T(8,128)S(1)}, u32[]{:S(2)}, u32[]{:S(2)}) async-start(f32[8,8,128]{2,1,0:T(8,128)} %join.1), calls=%async_computation.3 | async-start | bytes 65536 | tf_op jit(solution)/shard_map/all_to_all | solution.py:223
where the time goes:
time: 144 us; the launch traced here: 142 us
  starting transfers between devices  75.6 us (52%)
  waiting for transfers between devices  37.7 us (26%)
  Pallas kernels  23.4 us (16%)
  local copies, waits for them, and re-layouts  4 us (3%)
    all_to_all x4, starting transfers between devices, exchange(): return lax.all_to_all(value, axes, 0, 0)  37.5 us
    all_to_all x4, waiting for transfers between devices, exchange(): return lax.all_to_all(value, axes, 0, 0)  34.6 us
    ppermute x9, starting transfers between devices, turn(): return lax.ppermute(value, 'x', [(i, (i + k) % nx) for i in range(nx)])  29.4 us
    pallas_call x1, Pallas kernels, first_product(): pl.pallas_call(lambda *refs: first_kernel(wide_steps, *refs), grid=(steps...  10.6 us
    pallas_call x1, Pallas kernels, second_product(): pl.pallas_call(second_kernel, grid=(wide // TILE,), in_specs=[scalars(),...  9.16 us
    ppermute x1, starting transfers between devices, body(): other_weight = lax.ppermute(head_weight, 'c', [(0, 1), (1, 0)])  8.75 us
    ppermute x9, waiting for transfers between devices, turn(): return lax.ppermute(value, 'x', [(i, (i + k) % nx) for i in range(nx)])  3.18 us
  transfers between devices with their start and end apart: 14, of which 6 were waited for; matrix products, arithmetic and copies ran while one was open for 3% of the time, Pallas kernels for 8%

commit v1 on v0

v1 whole, which is shorter than its diff:
```python
import jax
import jax.numpy as jnp
from jax import lax
from jax.experimental import pallas as pl
from jax.experimental.pallas import tpu as pltpu
from jax.sharding import Mesh
from jax.sharding import PartitionSpec as P

WINDOW = 32
TOK_VOC = ("x", "c", "z", "y")
PLANE = ("z", "y")
WIDE = 3584
STRIP = 64
CHUNKS = 2
VMEM_LIMIT = 12 * 2**20
WIDE_VMEM = 20 * 2**20


def params(limit=8 * 2**20):
    return pltpu.CompilerParams(vmem_limit_bytes=limit)


def whole(shape):
    return pl.BlockSpec(shape, lambda *_: (0,) * len(shape))


def scalars():
    return pl.BlockSpec(memory_space=pltpu.SMEM)


def dot_t(a, b):
    return lax.dot_general(a, b, (((1,), (1,)), ((), ())), preferred_element_type=jnp.float32)


def norm_kernel(hidden, gain, wide, narrow):
    values = hidden[...].astype(jnp.float32)
    meansq = jnp.mean(values * values, axis=1, keepdims=True)
    normed = (values * lax.rsqrt(meansq + 1e-06) * gain[...].reshape(1, -1)).astype(jnp.bfloat16)
    width = wide.shape[2]
    narrow[...] = normed[:, width:]
    for i in range(wide.shape[0]):
        wide[i] = normed[:, :width]


def norm(hidden, gain, copies, width):
    rows, depth = hidden.shape
    shapes = [(copies, rows, width), (rows, depth - width)]
    return pl.pallas_call(
        norm_kernel,
        in_specs=[whole(hidden.shape), whole(gain.shape)],
        out_specs=[whole(s) for s in shapes],
        out_shape=[jax.ShapeDtypeStruct(s, jnp.bfloat16) for s in shapes],
        compiler_params=params(),
        name="norm",
    )(in_hbm(hidden), in_hbm(gain))


def wanted_of(place, targets, groups):
    rows = [targets[pl.ds(place[3 + k] * 2 + place[0], 1), :] for k in groups]
    return jnp.concatenate(rows, axis=1)


def token_sums(place, wanted, logits):
    vocab, tokens = logits.shape
    expsum = jnp.zeros((8, tokens), jnp.float32)
    picked = jnp.zeros((8, tokens), jnp.float32)
    column = lax.broadcasted_iota(jnp.int32, (STRIP, tokens), 0)
    for r in range(0, vocab, STRIP):
        shard, offset = divmod(r, vocab // 2)
        capped = 30.0 * jnp.tanh(logits[r:r + STRIP, :] / 30.0)
        hit = jnp.where(column == wanted - (place[1 + shard] + offset), capped, 0.0)
        expsum += jnp.sum(jnp.exp(capped).reshape(STRIP // 8, 8, tokens), axis=0)
        picked += jnp.sum(hit.reshape(STRIP // 8, 8, tokens), axis=0)
    return jnp.sum(expsum, axis=0, keepdims=True), jnp.sum(picked, axis=0, keepdims=True)


def fetch(shards, kept, sems, starts, width):
    vocab = shards[0].shape[0]
    copies = []
    for i, start in enumerate(starts):
        pair = []
        for j, shard in enumerate(shards):
            source = shard.at[:, start:start + width]
            target = kept.at[j * vocab:(j + 1) * vocab, start:start + width]
            pair.append(pltpu.make_async_copy(source, target, sems.at[2 * i + j]))
            pair[-1].start()
        copies.append(pair)
    return copies


def first_kernel(place, targets, x0, x1, x2, x3, mixed, w0, w1, late, stat, kept, rows, logits, narrow_w, sems):
    wide = x0.shape[1]
    tokens, _ = mixed.shape
    groups = tokens // 128
    early = logits.shape[1]
    half = tokens // 2
    vocab = w0.shape[0]
    copies = [
        pltpu.make_async_copy(w.at[:, wide:], narrow_w.at[j * vocab:(j + 1) * vocab, :], sems.at[2 * CHUNKS + j])
        for j, w in enumerate((w0, w1))
    ]
    for copy in copies:
        copy.start()
    width = wide // CHUNKS
    others = fetch((w0, w1), kept, sems, [i * width for i in range(CHUNKS)], width)
    row = lax.broadcasted_iota(jnp.int32, (half, half), 0)
    col = lax.broadcasted_iota(jnp.int32, (half, half), 1)
    inner = row & 63
    pick = (inner >> 1) * (2 * groups) + (row >> 6) * 2 + (inner & 1)
    chosen = jnp.where(col == pick, 1.0, 0.0).astype(jnp.bfloat16)
    for h in range(2):
        part = jnp.dot(chosen, mixed[h * half:(h + 1) * half, :], preferred_element_type=jnp.float32)
        for k in range(groups):
            rows[k * 128 + h * 64:k * 128 + h * 64 + 64, :] = part[k * 64:(k + 1) * 64].astype(jnp.bfloat16)
    for copy in copies:
        copy.wait()
    late[...] = dot_t(narrow_w[...], rows[early:, :])
    logits[...] = dot_t(narrow_w[...], rows[:early, :])
    for i in range(CHUNKS):
        for copy in others[i]:
            copy.wait()
        cols = slice(i * width, (i + 1) * width)
        x = jnp.concatenate([x0[:, cols], x1[:, cols], x2[:, cols], x3[:, cols]], axis=0)
        logits[...] += dot_t(kept[:, cols], x)
    sums = token_sums(place, wanted_of(place, targets, (0, 1)), logits)
    for i, total in enumerate(sums):
        for k in range(2):
            stat[2 * i + k:2 * i + k + 1, :] = total[:, k * 128:(k + 1) * 128]


def first_product(place, targets, xs, mixed, w0, w1):
    vocab, depth = 2 * w0.shape[0], w0.shape[1]
    tokens, narrow = mixed.shape
    early = sum(x.shape[0] for x in xs)
    inside = pl.BlockSpec(memory_space=pltpu.VMEM)
    outside = pl.BlockSpec(memory_space=pltpu.HBM)
    return pl.pallas_call(
        first_kernel,
        in_specs=[scalars()] + [inside] * 6 + [outside] * 2,
        out_specs=[inside] * 3,
        out_shape=[
            jax.ShapeDtypeStruct((vocab, tokens - early), jnp.float32),
            jax.ShapeDtypeStruct((8, 128), jnp.float32),
            jax.ShapeDtypeStruct((vocab, depth - narrow), w0.dtype),
        ],
        scratch_shapes=[
            pltpu.VMEM((tokens, narrow), jnp.bfloat16),
            pltpu.VMEM((vocab, early), jnp.float32),
            pltpu.VMEM((vocab, narrow), w0.dtype),
            pltpu.SemaphoreType.DMA((2 * CHUNKS + 2,)),
        ],
        compiler_params=params(WIDE_VMEM),
        cost_estimate=pl.CostEstimate(flops=vocab * tokens * depth, bytes_accessed=14 * 2**20, transcendentals=0),
        name="first_product",
    )(place, targets, *xs, mixed, w0, w1)


def second_kernel(place, targets, near, early_stat, x0, x1, x2, x3, weight, out, logits, stat):
    logits[...] = near[...] + dot_t(weight[...], jnp.concatenate([x0[...], x1[...], x2[...], x3[...]], axis=0))
    sums = token_sums(place, wanted_of(place, targets, (2, 3)), logits)
    for i, total in enumerate(sums):
        for k in range(2):
            stat[pl.ds(place[3 + k] + 4 * i, 1), :] = early_stat[2 * i + k:2 * i + k + 1, :]
            stat[pl.ds(place[5 + k] + 4 * i, 1), :] = total[:, k * 128:(k + 1) * 128]
    for i in range(out.shape[0]):
        out[i] = stat[...]


def second_product(place, targets, near, early_stat, xs, weight, copies):
    vocab, depth = weight.shape
    inside = pl.BlockSpec(memory_space=pltpu.VMEM)
    return pl.pallas_call(
        second_kernel,
        in_specs=[scalars()] + [inside] * 8,
        out_specs=inside,
        out_shape=jax.ShapeDtypeStruct((copies, *early_stat.shape), jnp.float32),
        scratch_shapes=[pltpu.VMEM(near.shape, jnp.float32), pltpu.VMEM(early_stat.shape, jnp.float32)],
        compiler_params=params(VMEM_LIMIT),
        cost_estimate=pl.CostEstimate(flops=2 * vocab * 256 * depth, bytes_accessed=10 * 2**20, transcendentals=0),
        name="second_product",
    )(place, targets, near, early_stat, *xs, weight)


def join_kernel(parts, out):
    total = jnp.sum(parts[...], axis=0)
    for i in range(out.shape[0]):
        out[i] = total


def join(parts, copies):
    shape = (copies, *parts.shape[1:])
    return pl.pallas_call(
        join_kernel,
        in_specs=[whole(parts.shape)],
        out_specs=whole(shape),
        out_shape=jax.ShapeDtypeStruct(shape, jnp.float32),
        compiler_params=params(),
        name="join",
    )(parts)


def loss_kernel(place, count, live, parts, token_loss, mean_loss, loss):
    groups = parts.shape[1] // 2
    for core in range(2):
        total = parts[core]
        for i in range(core + 2, parts.shape[0], 2):
            total = total + parts[i]
        rows = slice(core * groups, (core + 1) * groups)
        loss[rows, :] = live[rows, :] * (jnp.log(total[:groups]) - total[groups:])
    mean_loss[0] = jnp.sum(loss[...]) / count[0]
    own = loss[pl.ds(place[0], 1), :]
    lane = lax.broadcasted_iota(jnp.int32, own.shape, 1)
    for i in range(token_loss.shape[0]):
        token_loss[i] = jnp.sum(jnp.where(lane == place[1] + i, own, 0.0))


def final_loss(place, count, live, parts, own_rows):
    return pl.pallas_call(
        loss_kernel,
        in_specs=[scalars(), scalars(), whole(live.shape), whole(parts.shape)],
        out_specs=[scalars(), scalars()],
        out_shape=[jax.ShapeDtypeStruct((own_rows,), jnp.float32), jax.ShapeDtypeStruct((1,), jnp.float32)],
        scratch_shapes=[pltpu.VMEM(live.shape, jnp.float32)],
        compiler_params=params(),
        name="final_loss",
    )(place, count, live, parts)


def in_hbm(value):
    return pltpu.with_memory_space_constraint(value, pltpu.HBM)


def exchange(value, axes):
    return lax.all_to_all(value, axes, 0, 0)


def body(hidden, norm_gain, head_weight, targets, lengths):
    own_rows = hidden.shape[0]
    vocab_rows = head_weight.shape[0]
    nx, nc = lax.axis_size("x"), lax.axis_size("c")
    plane = lax.axis_size(PLANE)
    x, c = lax.axis_index("x"), lax.axis_index("c")
    seat = lax.axis_index(PLANE)
    block = plane * own_rows

    def turn(value, k):
        return lax.ppermute(value, "x", [(i, (i + k) % nx) for i in range(nx)])

    wide, narrow = norm(hidden, norm_gain, plane, WIDE)
    mine = exchange(wide, PLANE).reshape(block, WIDE)
    other_weight = lax.ppermute(head_weight, "c", [(0, 1), (1, 0)])
    column = jnp.concatenate([narrow, turn(narrow, 1), turn(narrow, nx - 1), turn(narrow, 2)], axis=0)
    mixed = exchange(jnp.broadcast_to(column[None], (plane, *column.shape)), PLANE).reshape(nx * block, -1)
    low, high = mine[:block // 2], mine[block // 2:]
    up_low, down_high = turn(low, 1), turn(high, nx - 1)
    up_high, down_low = turn(high, 1), turn(low, nx - 1)
    far_low, far_high = turn(up_low, 1), turn(down_high, nx - 1)
    sources = [lax.rem(x + nx - k, nx) for k in (0, 1, nx - 1, 2)]
    first = ((x * nc + c) * plane + seat) * vocab_rows
    second = ((x * nc + 1 - c) * plane + seat) * vocab_rows
    place = jnp.stack([c, first, second, *sources]).astype(jnp.int32)
    ids = targets.reshape(nx * nc, block)
    shards = in_hbm(head_weight), in_hbm(other_weight)
    near, early, weight = first_product(place, ids, (low, high, up_low, up_high), mixed, *shards)
    stats = second_product(place, ids, near, early, (down_low, down_high, far_low, far_high), weight, plane)
    stats = join(exchange(stats, PLANE), nx * nc)
    stats = exchange(stats, ("x", "c"))
    position = jnp.arange(WINDOW, dtype=jnp.int32)
    live = (position[None, :] < lengths[:, None]).astype(jnp.float32).reshape(nx, nc, block)
    live = live.transpose(1, 0, 2).reshape(nx * nc, block)
    count = jnp.sum(lengths.astype(jnp.float32)).reshape(1)
    seat_of = jnp.stack([c * nx + x, seat * own_rows]).astype(jnp.int32)
    token_loss, mean_loss = final_loss(seat_of, count, live, stats, own_rows)
    return (token_loss, mean_loss.reshape(()))


def solution(mesh):
    split = Mesh(mesh.devices.reshape(4, 2, 8, 8), TOK_VOC)
    in_specs = (P(TOK_VOC, None), P(), P(TOK_VOC, None), P(), P())
    out_specs = (P(TOK_VOC), P())
    return jax.shard_map(body, mesh=split, in_specs=in_specs, out_specs=out_specs, check_vma=False)
```

time: 144 us -> 138 us (0.958)
  Pallas kernels: 23.4 us -> 16.8 us
  starting transfers between devices: 75.6 us -> 77.1 us
  local copies, waits for them, and re-layouts: 4 us -> 2.54 us
    pallas_call x3, Pallas kernels: 20.9 us -> 14.3 us  [the longest x1 8.25 us: first_product(): pl.pallas_call(first_kernel, in_specs=[scalars()] + [inside] * 6 + [outsi...]
    all_to_all x4, starting transfers between devices: 37.5 us -> 38.9 us  [exchange(): return lax.all_to_all(value, axes, 0, 0)]
  transfers between devices with their start and end apart: 14 -> 14, of which waited for: 6 -> 7; matrix products, arithmetic and copies ran while one was open for 3% -> 2% of each run, Pallas kernels for 8% -> 7%
where the time goes in v1:
time: 138 us; the launch traced here: 137 us
  starting transfers between devices  77.1 us (56%)
  waiting for transfers between devices  38.7 us (28%)
  Pallas kernels  16.8 us (12%)
  local copies, waits for them, and re-layouts  2.54 us (2%)
    all_to_all x4, starting transfers between devices, exchange(): return lax.all_to_all(value, axes, 0, 0)  38.9 us
    all_to_all x4, waiting for transfers between devices, exchange(): return lax.all_to_all(value, axes, 0, 0)  34.5 us
    ppermute x9, starting transfers between devices, turn(): return lax.ppermute(value, 'x', [(i, (i + k) % nx) for i in range(nx)])  29.4 us
    ppermute x1, starting transfers between devices, body(): other_weight = lax.ppermute(head_weight, 'c', [(0, 1), (1, 0)])  8.75 us
    pallas_call x1, Pallas kernels, first_product(): pl.pallas_call(first_kernel, in_specs=[scalars()] + [inside] * 6 + [outsi...  8.25 us
    ppermute x9, waiting for transfers between devices, turn(): return lax.ppermute(value, 'x', [(i, (i + k) % nx) for i in range(nx)])  4.15 us
    pallas_call x1, Pallas kernels, second_product(): pl.pallas_call(second_kernel, in_specs=[scalars()] + [inside] * 8, out_sp...  4.14 us
  transfers between devices with their start and end apart: 14, of which 7 were waited for; matrix products, arithmetic and copies ran while one was open for 2% of the time, Pallas kernels for 7%

profile of v1, /device:TPU:1, one launch (start us, length us, event | category | flops | bytes accessed | tf_op | source)
XLA Modules:
  0.0 136.8 jit_solution(11603726547064913790)
XLA Ops:
  0.6 0.0 copy-start
  0.6 8.8 %collective-permute-start.5 = (bf16[512,4608]{1,0:T(8,128)(2,1)}, bf16[512,4608]{1,0:T(8,128)(2,1)}, u32[]{:S(2)}, u32[]{:S(2)}) collective-permute-start(bf16[512,4608]{1,0:T(8,128)(2,1)} %w0.1), channel_id=1, source_target_pairs={{0,64},{64,0},{1,65},{65,1},{2,66},{66,2},{3,67},{67,3},{4,68},{68... | collective-permute-start | bytes 14155784 | tf_op jit(solution)/shard_map/ppermute | solution.py:251
  9.4 1.9 %norm.1 = (bf16[64,2,3584]{2,1,0:T(2,128)(2,1)}, bf16[2,1024]{1,0:T(2,128)(2,1)S(1)}) custom-call(bf16[2,4608]{1,0:T(2,128)(2,1)} %hidden.1, f32[4608]{0:T(1024)} %gain.1), custom_call_target="tpu_custom_call" | custom-call | tf_op jit(solution)/shard_map/norm/pallas_call | solution.py:48
  11.3 11.0 %all-to-all-start = ((bf16[64,2,3584]{2,1,0:T(2,128)(2,1)}), bf16[64,2,3584]{2,1,0:T(2,128)(2,1)S(1)}, u32[]{:S(2)}, u32[]{:S(2)}) async-start(bf16[64,2,3584]{2,1,0:T(2,128)(2,1)} %get-tuple-element.9), calls=%async_computation | async-start | bytes 1835008 | tf_op jit(solution)/shard_map/all_to_all | solution.py:234
  22.3 3.1 %collective-permute-start.2 = (bf16[2,1024]{1,0:T(2,128)(2,1)S(1)}, bf16[2,1024]{1,0:T(2,128)(2,1)S(1)}, u32[]{:S(2)}, u32[]{:S(2)}) collective-permute-start(bf16[2,1024]{1,0:T(2,128)(2,1)S(1)} %get-tuple-element.10), channel_id=1, source_target_pairs={{0,128},{128,256},{256,384},{384,0},{1,129},{129,257},{257,385},{3... | collective-permute-start | bytes 12296 | tf_op jit(solution)/shard_map/ppermute | solution.py:247
  25.4 3.4 %collective-permute-start.3 = (bf16[2,1024]{1,0:T(2,128)(2,1)S(1)}, bf16[2,1024]{1,0:T(2,128)(2,1)S(1)}, u32[]{:S(2)}, u32[]{:S(2)}) collective-permute-start(bf16[2,1024]{1,0:T(2,128)(2,1)S(1)} %get-tuple-element.10), channel_id=1, source_target_pairs={{0,384},{128,0},{256,128},{384,256},{1,385},{129,1},{257,129},{385... | collective-permute-start | bytes 12296 | tf_op jit(solution)/shard_map/ppermute | solution.py:247
  28.8 3.4 %collective-permute-start.4 = (bf16[2,1024]{1,0:T(2,128)(2,1)S(1)}, bf16[2,1024]{1,0:T(2,128)(2,1)S(1)}, u32[]{:S(2)}, u32[]{:S(2)}) collective-permute-start(bf16[2,1024]{1,0:T(2,128)(2,1)S(1)} %get-tuple-element.10), channel_id=1, source_target_pairs={{0,256},{128,384},{256,0},{384,128},{1,257},{129,385},{257,1},{385... | collective-permute-start | bytes 12296 | tf_op jit(solution)/shard_map/ppermute | solution.py:247
  32.2 0.0 collective-permute-done.2
  32.2 0.0 collective-permute-done.3
  32.3 2.7 %collective-permute-done.4 = bf16[2,1024]{1,0:T(2,128)(2,1)S(1)} collective-permute-done((bf16[2,1024]{1,0:T(2,128)(2,1)S(1)}, bf16[2,1024]{1,0:T(2,128)(2,1)S(1)}, u32[]{:S(2)}, u32[]{:S(2)}) %collective-permute-start.4) | collective-permute-done | bytes 4128 | tf_op jit(solution)/shard_map/ppermute | solution.py:247
  35.0 12.7 %all-to-all-done = bf16[64,2,3584]{2,1,0:T(2,128)(2,1)S(1)} async-done(((bf16[64,2,3584]{2,1,0:T(2,128)(2,1)}), bf16[64,2,3584]{2,1,0:T(2,128)(2,1)S(1)}, u32[]{:S(2)}, u32[]{:S(2)}) %all-to-all-start) | async-done | bytes 917536 | tf_op jit(solution)/shard_map/all_to_all | solution.py:234
  47.7 1.1 broadcast_in_dim.2
  48.8 7.5 %all-to-all-start.1 = ((bf16[64,8,1024]{2,1,0:T(8,128)(2,1)}), bf16[64,8,1024]{2,1,0:T(8,128)(2,1)S(1)}, u32[]{:S(2)}, u32[]{:S(2)}) async-start(bf16[64,8,1024]{2,1,0:T(8,128)(2,1)} %broadcast_in_dim.2), calls=%async_computation.1 | async-start | bytes 2097152 | tf_op jit(solution)/shard_map/all_to_all | solution.py:234
  56.4 0.6 fusion
  57.0 0.2 slice.13.x0
  57.2 3.1 %collective-permute-start = (bf16[64,3584]{1,0:T(8,128)(2,1)S(1)}, bf16[64,3584]{1,0:T(8,128)(2,1)S(1)}, u32[]{:S(2)}, u32[]{:S(2)}) collective-permute-start(bf16[64,3584]{1,0:T(8,128)(2,1)S(1)} %slice.13.x0), channel_id=1, source_target_pairs={{0,128},{128,256},{256,384},{384,0},{1,129},{129,257},{257,385},{3... | collective-permute-start | bytes 1376264 | tf_op jit(solution)/shard_map/ppermute | solution.py:247
  60.3 0.2 slice.15.x1
  60.5 3.4 %collective-permute-start.7 = (bf16[64,3584]{1,0:T(8,128)(2,1)S(1)}, bf16[64,3584]{1,0:T(8,128)(2,1)S(1)}, u32[]{:S(2)}, u32[]{:S(2)}) collective-permute-start(bf16[64,3584]{1,0:T(8,128)(2,1)S(1)} %slice.15.x1), channel_id=1, source_target_pairs={{0,384},{128,0},{256,128},{384,256},{1,385},{129,1},{257,129},{385... | collective-permute-start | bytes 1376264 | tf_op jit(solution)/shard_map/ppermute | solution.py:247
  63.9 1.9 %collective-permute-start.1 = (bf16[64,3584]{1,0:T(8,128)(2,1)S(1)}, bf16[64,3584]{1,0:T(8,128)(2,1)}, u32[]{:S(2)}, u32[]{:S(2)}) collective-permute-start(bf16[64,3584]{1,0:T(8,128)(2,1)S(1)} %slice.15.x1), channel_id=1, source_target_pairs={{0,128},{128,256},{256,384},{384,0},{1,129},{129,257},{257,385},{3... | collective-permute-start | bytes 1376264 | tf_op jit(solution)/shard_map/ppermute | solution.py:247
  65.8 4.6 %collective-permute-start.6 = (bf16[64,3584]{1,0:T(8,128)(2,1)S(1)}, bf16[64,3584]{1,0:T(8,128)(2,1)S(1)}, u32[]{:S(2)}, u32[]{:S(2)}) collective-permute-start(bf16[64,3584]{1,0:T(8,128)(2,1)S(1)} %slice.13.x0), channel_id=1, source_target_pairs={{0,384},{128,0},{256,128},{384,256},{1,385},{129,1},{257,129},{385... | collective-permute-start | bytes 1376264 | tf_op jit(solution)/shard_map/ppermute | solution.py:247
  70.4 0.5 collective-permute-done.x2
  70.9 1.9 %collective-permute-start.8 = (bf16[64,3584]{1,0:T(8,128)(2,1)S(1)}, bf16[64,3584]{1,0:T(8,128)(2,1)}, u32[]{:S(2)}, u32[]{:S(2)}) collective-permute-start(bf16[64,3584]{1,0:T(8,128)(2,1)S(1)} %collective-permute-done.x2), channel_id=1, source_target_pairs={{0,128},{128,256},{256,384},{384,0},{1,129},{129,257},{257,385},{3... | collective-permute-start | bytes 1376264 | tf_op jit(solution)/shard_map/ppermute | solution.py:247
  72.8 0.0 collective-permute-done.7.x1
  72.8 4.6 %collective-permute-start.9 = (bf16[64,3584]{1,0:T(8,128)(2,1)S(1)}, bf16[64,3584]{1,0:T(8,128)(2,1)}, u32[]{:S(2)}, u32[]{:S(2)}) collective-permute-start(bf16[64,3584]{1,0:T(8,128)(2,1)S(1)} %collective-permute-done.7.x1), channel_id=1, source_target_pairs={{0,384},{128,0},{256,128},{384,256},{1,385},{129,1},{257,129},{385... | collective-permute-start | bytes 1376264 | tf_op jit(solution)/shard_map/ppermute | solution.py:247
  77.4 0.1 stack.43.place
  77.5 5.7 %all-to-all-done.1 = bf16[64,8,1024]{2,1,0:T(8,128)(2,1)S(1)} async-done(((bf16[64,8,1024]{2,1,0:T(8,128)(2,1)}), bf16[64,8,1024]{2,1,0:T(8,128)(2,1)S(1)}, u32[]{:S(2)}, u32[]{:S(2)}) %all-to-all-start.1) | async-done | bytes 1048608 | tf_op jit(solution)/shard_map/all_to_all | solution.py:234
  83.2 0.0 collective-permute-done.1.x3
  83.2 0.0 collective-permute-done.5.w1
  83.2 0.0 copy-done
  83.2 8.3 %first_product.1 = (f32[1024,256]{1,0:T(8,128)S(1)}, f32[8,128]{1,0:T(8,128)S(1)}, bf16[1024,3584]{1,0:T(8,128)(2,1)S(1)}) custom-call(s32[7]{0:T(128)S(1)} %stack.43.place, s32[8,128]{1,0:T(8,128)S(1)} %bitcast.19, bf16[64,3584]{1,0:T(8,128)(2,1)S(1)} %slice.13.x0, bf16[64,3584]{1,0:T(8,128)(2,1)S(1)} %slice.15.x1, ...), custom_call_target="tpu_custom_call" | custom-call | flops 2415919104 | bytes 14680064 | tf_op jit(solution)/shard_map/first_product/pallas_call | solution.py:137
  91.5 0.0 collective-permute-done.6.x0
  91.5 0.0 collective-permute-done.8.x2
  91.5 1.0 collective-permute-done.9.x3
  92.5 0.0 copy-start.1
  92.5 4.1 %second_product.1 = f32[64,8,128]{2,1,0:T(8,128)} custom-call(s32[7]{0:T(128)S(1)} %stack.43.place, s32[8,128]{1,0:T(8,128)S(1)} %bitcast.20, f32[1024,256]{1,0:T(8,128)S(1)} %get-tuple-element.11.near, f32[8,128]{1,0:T(8,128)S(1)} %get-tuple-element.12.early_stat, bf16[64,3584]{1,0:T(8,128)(2,1)S(1)} %collective-permute-done.6.x0, ...), custom_call_target="tpu_custom_call" | custom-call | flops 1879048192 | bytes 10485760 | tf_op jit(solution)/shard_map/second_product/pallas_call | solution.py:172
  96.6 11.9 %all-to-all-start.2 = ((f32[64,8,128]{2,1,0:T(8,128)}), f32[64,8,128]{2,1,0:T(8,128)S(1)}, u32[]{:S(2)}, u32[]{:S(2)}) async-start(f32[64,8,128]{2,1,0:T(8,128)} %second_product.1), calls=%async_computation.2 | async-start | bytes 524288 | tf_op jit(solution)/shard_map/all_to_all | solution.py:234
  108.5 0.0 copy-done.1
  108.5 0.1 lt.25
  108.6 0.1 lt.26
  108.6 0.1 lt.27
  108.7 0.1 lt.23
  108.8 0.7 convert_reduce_fusion
  109.5 11.4 %all-to-all-done.2.parts = f32[64,8,128]{2,1,0:T(8,128)S(1)} async-done(((f32[64,8,128]{2,1,0:T(8,128)}), f32[64,8,128]{2,1,0:T(8,128)S(1)}, u32[]{:S(2)}, u32[]{:S(2)}) %all-to-all-start.2) | async-done | bytes 262176 | tf_op jit(solution)/shard_map/all_to_all | solution.py:234
  120.9 0.7 join.1
  121.6 8.6 %all-to-all-start.3 = ((f32[8,8,128]{2,1,0:T(8,128)}), f32[8,8,128]{2,1,0:T(8,128)S(1)}, u32[]{:S(2)}, u32[]{:S(2)}) async-start(f32[8,8,128]{2,1,0:T(8,128)} %join.1), calls=%async_computation.3 | async-start | bytes 65536 | tf_op jit(solution)/shard_map/all_to_all | solution.py:234
  130.2 0.1 pad_add_fusion.place
  130.3 4.6 %all-to-all-done.3.parts = f32[8,8,128]{2,1,0:T(8,128)S(1)} async-done(((f32[8,8,128]{2,1,0:T(8,128)}), f32[8,8,128]{2,1,0:T(8,128)S(1)}, u32[]{:S(2)}, u32[]{:S(2)}) %all-to-all-start.3) | async-done | bytes 32800 | tf_op jit(solution)/shard_map/all_to_all | solution.py:234
  134.9 1.9 %final_loss.1 = (f32[2]{0:T(128)}, f32[1]{0:T(128)}) custom-call(s32[2]{0:T(128)S(1)} %pad_add_fusion.place, f32[1]{0:T(128)} %bitcast.2.count, f32[8,128]{1,0:T(8,128)S(1)} %bitcast.21, f32[8,8,128]{2,1,0:T(8,128)S(1)} %all-to-all-done.3.parts), custom_call_target="tpu_custom_call" | custom-call | tf_op jit(solution)/shard_map/final_loss/pallas_call | solution.py:218
  (4 shorter events, 0.0 us)
Async XLA Ops:
  0.6 82.6 %copy-start = (s32[1024]{0:T(1024)S(1)}, s32[1024]{0:T(1024)}, u32[]{:S(2)}) copy-start(s32[1024]{0:T(1024)} %param.8) | copy-start | bytes 12292
  0.6 82.6 %collective-permute-start.5 = (bf16[512,4608]{1,0:T(8,128)(2,1)}, bf16[512,4608]{1,0:T(8,128)(2,1)}, u32[]{:S(2)}, u32[]{:S(2)}) collective-permute-start(bf16[512,4608]{1,0:T(8,128)(2,1)} %w0.1), channel_id=1, source_target_pairs={{0,64},{64,0},{1,65},{65,1},{2,66},{66,2},{3,67},{67,3},{4,68},{68... | collective-permute-start | bytes 14155784 | tf_op jit(solution)/shard_map/ppermute | solution.py:251
  11.3 36.4 %all-to-all-start = ((bf16[64,2,3584]{2,1,0:T(2,128)(2,1)}), bf16[64,2,3584]{2,1,0:T(2,128)(2,1)S(1)}, u32[]{:S(2)}, u32[]{:S(2)}) async-start(bf16[64,2,3584]{2,1,0:T(2,128)(2,1)} %get-tuple-element.9), calls=%async_computation | async-start | bytes 1835008 | tf_op jit(solution)/shard_map/all_to_all | solution.py:234
  22.3 10.0 %collective-permute-start.2 = (bf16[2,1024]{1,0:T(2,128)(2,1)S(1)}, bf16[2,1024]{1,0:T(2,128)(2,1)S(1)}, u32[]{:S(2)}, u32[]{:S(2)}) collective-permute-start(bf16[2,1024]{1,0:T(2,128)(2,1)S(1)} %get-tuple-element.10), channel_id=1, source_target_pairs={{0,128},{128,256},{256,384},{384,0},{1,129},{129,257},{257,385},{3... | collective-permute-start | bytes 12296 | tf_op jit(solution)/shard_map/ppermute | solution.py:247
  25.4 6.8 %collective-permute-start.3 = (bf16[2,1024]{1,0:T(2,128)(2,1)S(1)}, bf16[2,1024]{1,0:T(2,128)(2,1)S(1)}, u32[]{:S(2)}, u32[]{:S(2)}) collective-permute-start(bf16[2,1024]{1,0:T(2,128)(2,1)S(1)} %get-tuple-element.10), channel_id=1, source_target_pairs={{0,384},{128,0},{256,128},{384,256},{1,385},{129,1},{257,129},{385... | collective-permute-start | bytes 12296 | tf_op jit(solution)/shard_map/ppermute | solution.py:247
  28.8 6.2 %collective-permute-start.4 = (bf16[2,1024]{1,0:T(2,128)(2,1)S(1)}, bf16[2,1024]{1,0:T(2,128)(2,1)S(1)}, u32[]{:S(2)}, u32[]{:S(2)}) collective-permute-start(bf16[2,1024]{1,0:T(2,128)(2,1)S(1)} %get-tuple-element.10), channel_id=1, source_target_pairs={{0,256},{128,384},{256,0},{384,128},{1,257},{129,385},{257,1},{385... | collective-permute-start | bytes 12296 | tf_op jit(solution)/shard_map/ppermute | solution.py:247
  48.8 34.4 %all-to-all-start.1 = ((bf16[64,8,1024]{2,1,0:T(8,128)(2,1)}), bf16[64,8,1024]{2,1,0:T(8,128)(2,1)S(1)}, u32[]{:S(2)}, u32[]{:S(2)}) async-start(bf16[64,8,1024]{2,1,0:T(8,128)(2,1)} %broadcast_in_dim.2), calls=%async_computation.1 | async-start | bytes 2097152 | tf_op jit(solution)/shard_map/all_to_all | solution.py:234
  57.2 13.7 %collective-permute-start = (bf16[64,3584]{1,0:T(8,128)(2,1)S(1)}, bf16[64,3584]{1,0:T(8,128)(2,1)S(1)}, u32[]{:S(2)}, u32[]{:S(2)}) collective-permute-start(bf16[64,3584]{1,0:T(8,128)(2,1)S(1)} %slice.13.x0), channel_id=1, source_target_pairs={{0,128},{128,256},{256,384},{384,0},{1,129},{129,257},{257,385},{3... | collective-permute-start | bytes 1376264 | tf_op jit(solution)/shard_map/ppermute | solution.py:247
  60.5 12.3 %collective-permute-start.7 = (bf16[64,3584]{1,0:T(8,128)(2,1)S(1)}, bf16[64,3584]{1,0:T(8,128)(2,1)S(1)}, u32[]{:S(2)}, u32[]{:S(2)}) collective-permute-start(bf16[64,3584]{1,0:T(8,128)(2,1)S(1)} %slice.15.x1), channel_id=1, source_target_pairs={{0,384},{128,0},{256,128},{384,256},{1,385},{129,1},{257,129},{385... | collective-permute-start | bytes 1376264 | tf_op jit(solution)/shard_map/ppermute | solution.py:247
  63.9 19.3 %collective-permute-start.1 = (bf16[64,3584]{1,0:T(8,128)(2,1)S(1)}, bf16[64,3584]{1,0:T(8,128)(2,1)}, u32[]{:S(2)}, u32[]{:S(2)}) collective-permute-start(bf16[64,3584]{1,0:T(8,128)(2,1)S(1)} %slice.15.x1), channel_id=1, source_target_pairs={{0,128},{128,256},{256,384},{384,0},{1,129},{129,257},{257,385},{3... | collective-permute-start | bytes 1376264 | tf_op jit(solution)/shard_map/ppermute | solution.py:247
  65.8 25.7 %collective-permute-start.6 = (bf16[64,3584]{1,0:T(8,128)(2,1)S(1)}, bf16[64,3584]{1,0:T(8,128)(2,1)S(1)}, u32[]{:S(2)}, u32[]{:S(2)}) collective-permute-start(bf16[64,3584]{1,0:T(8,128)(2,1)S(1)} %slice.13.x0), channel_id=1, source_target_pairs={{0,384},{128,0},{256,128},{384,256},{1,385},{129,1},{257,129},{385... | collective-permute-start | bytes 1376264 | tf_op jit(solution)/shard_map/ppermute | solution.py:247
  70.9 20.6 %collective-permute-start.8 = (bf16[64,3584]{1,0:T(8,128)(2,1)S(1)}, bf16[64,3584]{1,0:T(8,128)(2,1)}, u32[]{:S(2)}, u32[]{:S(2)}) collective-permute-start(bf16[64,3584]{1,0:T(8,128)(2,1)S(1)} %collective-permute-done.x2), channel_id=1, source_target_pairs={{0,128},{128,256},{256,384},{384,0},{1,129},{129,257},{257,385},{3... | collective-permute-start | bytes 1376264 | tf_op jit(solution)/shard_map/ppermute | solution.py:247
  72.8 19.7 %collective-permute-start.9 = (bf16[64,3584]{1,0:T(8,128)(2,1)S(1)}, bf16[64,3584]{1,0:T(8,128)(2,1)}, u32[]{:S(2)}, u32[]{:S(2)}) collective-permute-start(bf16[64,3584]{1,0:T(8,128)(2,1)S(1)} %collective-permute-done.7.x1), channel_id=1, source_target_pairs={{0,384},{128,0},{256,128},{384,256},{1,385},{129,1},{257,129},{385... | collective-permute-start | bytes 1376264 | tf_op jit(solution)/shard_map/ppermute | solution.py:247
  92.5 16.0 %copy-start.1 = (s32[32]{0:T(128)S(1)}, s32[32]{0:T(128)}, u32[]{:S(2)}) copy-start(s32[32]{0:T(128)} %param.9) | copy-start | bytes 388
  96.6 24.3 %all-to-all-start.2 = ((f32[64,8,128]{2,1,0:T(8,128)}), f32[64,8,128]{2,1,0:T(8,128)S(1)}, u32[]{:S(2)}, u32[]{:S(2)}) async-start(f32[64,8,128]{2,1,0:T(8,128)} %second_product.1), calls=%async_computation.2 | async-start | bytes 524288 | tf_op jit(solution)/shard_map/all_to_all | solution.py:234
  121.6 13.3 %all-to-all-start.3 = ((f32[8,8,128]{2,1,0:T(8,128)}), f32[8,8,128]{2,1,0:T(8,128)S(1)}, u32[]{:S(2)}, u32[]{:S(2)}) async-start(f32[8,8,128]{2,1,0:T(8,128)} %join.1), calls=%async_computation.3 | async-start | bytes 65536 | tf_op jit(solution)/shard_map/all_to_all | solution.py:234

commit v2 on v1

--- a/solution.py
+++ b/solution.py
@@ -55,20 +55,31 @@
     )(in_hbm(hidden), in_hbm(gain))
 
 
-def wanted_of(place, targets, groups):
-    rows = [targets[pl.ds(place[3 + k] * 2 + place[0], 1), :] for k in groups]
-    return jnp.concatenate(rows, axis=1)
-
-
-def token_sums(place, wanted, logits):
+def position(own_rows):
+    x, c = lax.axis_index("x"), lax.axis_index("c")
+    seat = lax.axis_index("z") * lax.axis_size("y") + lax.axis_index("y")
+    return x, c, seat * own_rows
+
+
+def sources(x):
+    nx = lax.axis_size("x")
+    return [lax.rem(x + nx - k, nx) for k in (0, 1, nx - 1, 2)]
+
+
+def token_sums(targets, groups, logits):
     vocab, tokens = logits.shape
+    shard = vocab // 2
+    x, c, seat = position(1)
+    nc, plane = lax.axis_size("c"), lax.axis_size(PLANE)
+    starts = [((x * nc + core) * plane + seat) * shard for core in (c, 1 - c)]
+    wanted = jnp.concatenate([targets[pl.ds(sources(x)[k] * nc + c, 1), :] for k in groups], axis=1)
     expsum = jnp.zeros((8, tokens), jnp.float32)
     picked = jnp.zeros((8, tokens), jnp.float32)
     column = lax.broadcasted_iota(jnp.int32, (STRIP, tokens), 0)
     for r in range(0, vocab, STRIP):
-        shard, offset = divmod(r, vocab // 2)
+        half, offset = divmod(r, shard)
         capped = 30.0 * jnp.tanh(logits[r:r + STRIP, :] / 30.0)
-        hit = jnp.where(column == wanted - (place[1 + shard] + offset), capped, 0.0)
+        hit = jnp.where(column == wanted - (starts[half] + offset), capped, 0.0)
         expsum += jnp.sum(jnp.exp(capped).reshape(STRIP // 8, 8, tokens), axis=0)
         picked += jnp.sum(hit.reshape(STRIP // 8, 8, tokens), axis=0)
     return jnp.sum(expsum, axis=0, keepdims=True), jnp.sum(picked, axis=0, keepdims=True)
@@ -88,9 +99,11 @@
     return copies
 
 
-def first_kernel(place, targets, x0, x1, x2, x3, mixed, w0, w1, late, stat, kept, rows, logits, narrow_w, sems):
+def first_kernel(
+    lengths, targets, x0, x1, x2, x3, mixed, w0, w1, late, stat, live, kept, rows, logits, narrow_w, sems
+):
     wide = x0.shape[1]
-    tokens, _ = mixed.shape
+    tokens = mixed.shape[0]
     groups = tokens // 128
     early = logits.shape[1]
     half = tokens // 2
@@ -103,6 +116,18 @@
         copy.start()
     width = wide // CHUNKS
     others = fetch((w0, w1), kept, sems, [i * width for i in range(CHUNKS)], width)
+    lane = lax.broadcasted_iota(jnp.int32, (1, 128), 1)
+    count = 0
+    for core in range(2):
+        for k in range(groups):
+            length = jnp.zeros((1, 128), jnp.int32)
+            for j in range(128 // WINDOW):
+                here = lengths[(k * 2 + core) * (128 // WINDOW) + j]
+                count = count + here
+                length = jnp.where(lane // WINDOW == j, here, length)
+            i = core * groups + k
+            live[i:i + 1, :] = jnp.where(lane % WINDOW < length, 1.0, 0.0)
+    live[2 * groups:, :] = jnp.full((2 * groups, 128), count, jnp.int32).astype(jnp.float32)
     row = lax.broadcasted_iota(jnp.int32, (half, half), 0)
     col = lax.broadcasted_iota(jnp.int32, (half, half), 1)
     inner = row & 63
@@ -122,25 +147,26 @@
         cols = slice(i * width, (i + 1) * width)
         x = jnp.concatenate([x0[:, cols], x1[:, cols], x2[:, cols], x3[:, cols]], axis=0)
         logits[...] += dot_t(kept[:, cols], x)
-    sums = token_sums(place, wanted_of(place, targets, (0, 1)), logits)
-    for i, total in enumerate(sums):
+    for i, total in enumerate(token_sums(targets, (0, 1), logits)):
         for k in range(2):
             stat[2 * i + k:2 * i + k + 1, :] = total[:, k * 128:(k + 1) * 128]
 
 
-def first_product(place, targets, xs, mixed, w0, w1):
+INSIDE = pl.BlockSpec(memory_space=pltpu.VMEM)
+
+
+def first_product(lengths, targets, xs, mixed, w0, w1):
     vocab, depth = 2 * w0.shape[0], w0.shape[1]
     tokens, narrow = mixed.shape
     early = sum(x.shape[0] for x in xs)
-    inside = pl.BlockSpec(memory_space=pltpu.VMEM)
-    outside = pl.BlockSpec(memory_space=pltpu.HBM)
     return pl.pallas_call(
         first_kernel,
-        in_specs=[scalars()] + [inside] * 6 + [outside] * 2,
-        out_specs=[inside] * 3,
+        in_specs=[scalars()] + [INSIDE] * 6 + [pl.BlockSpec(memory_space=pltpu.HBM)] * 2,
+        out_specs=[INSIDE] * 4,
         out_shape=[
             jax.ShapeDtypeStruct((vocab, tokens - early), jnp.float32),
             jax.ShapeDtypeStruct((8, 128), jnp.float32),
+            jax.ShapeDtypeStruct((16, 128), jnp.float32),
             jax.ShapeDtypeStruct((vocab, depth - narrow), w0.dtype),
         ],
         scratch_shapes=[
@@ -152,33 +178,32 @@
         compiler_params=params(WIDE_VMEM),
         cost_estimate=pl.CostEstimate(flops=vocab * tokens * depth, bytes_accessed=14 * 2**20, transcendentals=0),
         name="first_product",
-    )(place, targets, *xs, mixed, w0, w1)
-
-
-def second_kernel(place, targets, near, early_stat, x0, x1, x2, x3, weight, out, logits, stat):
-    logits[...] = near[...] + dot_t(weight[...], jnp.concatenate([x0[...], x1[...], x2[...], x3[...]], axis=0))
-    sums = token_sums(place, wanted_of(place, targets, (2, 3)), logits)
-    for i, total in enumerate(sums):
+    )(lengths, targets, *xs, mixed, w0, w1)
+
+
+def last_kernel(targets, late, early_stat, x0, x1, x2, x3, weight, out, logits, stat):
+    logits[...] = late[...] + dot_t(weight[...], jnp.concatenate([x0[...], x1[...], x2[...], x3[...]], axis=0))
+    origin = sources(lax.axis_index("x"))
+    for i, total in enumerate(token_sums(targets, (2, 3), logits)):
         for k in range(2):
-            stat[pl.ds(place[3 + k] + 4 * i, 1), :] = early_stat[2 * i + k:2 * i + k + 1, :]
-            stat[pl.ds(place[5 + k] + 4 * i, 1), :] = total[:, k * 128:(k + 1) * 128]
+            stat[pl.ds(origin[k] + 4 * i, 1), :] = early_stat[2 * i + k:2 * i + k + 1, :]
+            stat[pl.ds(origin[2 + k] + 4 * i, 1), :] = total[:, k * 128:(k + 1) * 128]
     for i in range(out.shape[0]):
         out[i] = stat[...]
 
 
-def second_product(place, targets, near, early_stat, xs, weight, copies):
+def last_product(targets, late, early_stat, xs, weight, copies):
     vocab, depth = weight.shape
-    inside = pl.BlockSpec(memory_space=pltpu.VMEM)
-    return pl.pallas_call(
-        second_kernel,
-        in_specs=[scalars()] + [inside] * 8,
-        out_specs=inside,
+    return pl.pallas_call(
+        last_kernel,
+        in_specs=[INSIDE] * 8,
+        out_specs=INSIDE,
         out_shape=jax.ShapeDtypeStruct((copies, *early_stat.shape), jnp.float32),
-        scratch_shapes=[pltpu.VMEM(near.shape, jnp.float32), pltpu.VMEM(early_stat.shape, jnp.float32)],
+        scratch_shapes=[pltpu.VMEM(late.shape, jnp.float32), pltpu.VMEM(early_stat.shape, jnp.float32)],
         compiler_params=params(VMEM_LIMIT),
         cost_estimate=pl.CostEstimate(flops=2 * vocab * 256 * depth, bytes_accessed=10 * 2**20, transcendentals=0),
-        name="second_product",
-    )(place, targets, near, early_stat, *xs, weight)
+        name="last_product",
+    )(targets, late, early_stat, *xs, weight)
 
 
 def join_kernel(parts, out):
@@ -188,18 +213,17 @@
 
 
 def join(parts, copies):
-    shape = (copies, *parts.shape[1:])
     return pl.pallas_call(
         join_kernel,
-        in_specs=[whole(parts.shape)],
-        out_specs=whole(shape),
-        out_shape=jax.ShapeDtypeStruct(shape, jnp.float32),
+        in_specs=[INSIDE],
+        out_specs=INSIDE,
+        out_shape=jax.ShapeDtypeStruct((copies, *parts.shape[1:]), jnp.float32),
         compiler_params=params(),
         name="join",
     )(parts)
 
 
-def loss_kernel(place, count, live, parts, token_loss, mean_loss, loss):
+def loss_kernel(live, parts, token_loss, mean_loss, loss):
     groups = parts.shape[1] // 2
     for core in range(2):
         total = parts[core]
@@ -207,23 +231,25 @@
             total = total + parts[i]
         rows = slice(core * groups, (core + 1) * groups)
         loss[rows, :] = live[rows, :] * (jnp.log(total[:groups]) - total[groups:])
-    mean_loss[0] = jnp.sum(loss[...]) / count[0]
-    own = loss[pl.ds(place[0], 1), :]
+    mean_loss[0] = jnp.sum(loss[...]) / live[2 * groups, 0]
+    own_rows = token_loss.shape[0]
+    x, c, seat = position(own_rows)
+    own = loss[pl.ds(c * groups + x, 1), :]
     lane = lax.broadcasted_iota(jnp.int32, own.shape, 1)
-    for i in range(token_loss.shape[0]):
-        token_loss[i] = jnp.sum(jnp.where(lane == place[1] + i, own, 0.0))
-
-
-def final_loss(place, count, live, parts, own_rows):
+    for i in range(own_rows):
+        token_loss[i] = jnp.sum(jnp.where(lane == seat + i, own, 0.0))
+
+
+def final_loss(live, parts, own_rows):
     return pl.pallas_call(
         loss_kernel,
-        in_specs=[scalars(), scalars(), whole(live.shape), whole(parts.shape)],
+        in_specs=[INSIDE] * 2,
         out_specs=[scalars(), scalars()],
         out_shape=[jax.ShapeDtypeStruct((own_rows,), jnp.float32), jax.ShapeDtypeStruct((1,), jnp.float32)],
-        scratch_shapes=[pltpu.VMEM(live.shape, jnp.float32)],
+        scratch_shapes=[pltpu.VMEM(parts.shape[1:], jnp.float32)],
         compiler_params=params(),
         name="final_loss",
-    )(place, count, live, parts)
+    )(live, parts)
 
 
 def in_hbm(value):
@@ -236,11 +262,8 @@
 
 def body(hidden, norm_gain, head_weight, targets, lengths):
     own_rows = hidden.shape[0]
-    vocab_rows = head_weight.shape[0]
     nx, nc = lax.axis_size("x"), lax.axis_size("c")
     plane = lax.axis_size(PLANE)
-    x, c = lax.axis_index("x"), lax.axis_index("c")
-    seat = lax.axis_index(PLANE)
     block = plane * own_rows
 
     def turn(value, k):
@@ -255,22 +278,13 @@
     up_low, down_high = turn(low, 1), turn(high, nx - 1)
     up_high, down_low = turn(high, 1), turn(low, nx - 1)
     far_low, far_high = turn(up_low, 1), turn(down_high, nx - 1)
-    sources = [lax.rem(x + nx - k, nx) for k in (0, 1, nx - 1, 2)]
-    first = ((x * nc + c) * plane + seat) * vocab_rows
-    second = ((x * nc + 1 - c) * plane + seat) * vocab_rows
-    place = jnp.stack([c, first, second, *sources]).astype(jnp.int32)
     ids = targets.reshape(nx * nc, block)
     shards = in_hbm(head_weight), in_hbm(other_weight)
-    near, early, weight = first_product(place, ids, (low, high, up_low, up_high), mixed, *shards)
-    stats = second_product(place, ids, near, early, (down_low, down_high, far_low, far_high), weight, plane)
+    late, early, live, wide_w = first_product(lengths, ids, (low, high, up_low, up_high), mixed, *shards)
+    stats = last_product(ids, late, early, (down_low, down_high, far_low, far_high), wide_w, plane)
     stats = join(exchange(stats, PLANE), nx * nc)
     stats = exchange(stats, ("x", "c"))
-    position = jnp.arange(WINDOW, dtype=jnp.int32)
-    live = (position[None, :] < lengths[:, None]).astype(jnp.float32).reshape(nx, nc, block)
-    live = live.transpose(1, 0, 2).reshape(nx * nc, block)
-    count = jnp.sum(lengths.astype(jnp.float32)).reshape(1)
-    seat_of = jnp.stack([c * nx + x, seat * own_rows]).astype(jnp.int32)
-    token_loss, mean_loss = final_loss(seat_of, count, live, stats, own_rows)
+    token_loss, mean_loss = final_loss(live, stats, own_rows)
     return (token_loss, mean_loss.reshape(()))
 
 

time: 138 us -> 135 us (0.978)
  blocking collectives: 0 us -> 37.2 us
  starting transfers between devices: 77.1 us -> 56.8 us
  waiting for transfers between devices: 38.7 us -> 22.7 us
  Pallas kernels: 16.8 us -> 14.4 us
    all_to_all x0 -> x2, blocking collectives: none -> 37.2 us  [exchange(): return lax.all_to_all(value, axes, 0, 0)]
    all_to_all x4 -> x2, starting transfers between devices: 38.9 us -> 18.5 us  [exchange(): return lax.all_to_all(value, axes, 0, 0)]
    all_to_all x4 -> x2, waiting for transfers between devices: 34.5 us -> 18.5 us  [exchange(): return lax.all_to_all(value, axes, 0, 0)]
    pallas_call x4, Pallas kernels: 14.9 us -> 12.5 us  [the longest x1 8.27 us: first_product(): pl.pallas_call(first_kernel, in_specs=[scalars()] + [INSIDE] * 6 + [pl.Bl...]
  transfers between devices with their start and end apart: 14 -> 12, of which waited for: 7 -> 5; matrix products, arithmetic and copies ran while one was open for 2% -> 2% of each run, Pallas kernels for 7% -> 8%
where the time goes in v2:
time: 135 us; the launch traced here: 134 us
  starting transfers between devices  56.8 us (42%)
  blocking collectives  37.2 us (28%)
  waiting for transfers between devices  22.7 us (17%)
  Pallas kernels  14.4 us (11%)
  local copies, waits for them, and re-layouts  2.12 us (2%)
    all_to_all x2, blocking collectives, exchange(): return lax.all_to_all(value, axes, 0, 0)  37.2 us
    ppermute x9, starting transfers between devices, turn(): return lax.ppermute(value, 'x', [(i, (i + k) % nx) for i in range(nx)])  29.4 us
    all_to_all x2, waiting for transfers between devices, exchange(): return lax.all_to_all(value, axes, 0, 0)  18.5 us
    all_to_all x2, starting transfers between devices, exchange(): return lax.all_to_all(value, axes, 0, 0)  18.5 us
    ppermute x1, starting transfers between devices, body(): other_weight = lax.ppermute(head_weight, 'c', [(0, 1), (1, 0)])  8.88 us
    pallas_call x1, Pallas kernels, first_product(): pl.pallas_call(first_kernel, in_specs=[scalars()] + [INSIDE] * 6 + [pl.Bl...  8.27 us
    ppermute x9, waiting for transfers between devices, turn(): return lax.ppermute(value, 'x', [(i, (i + k) % nx) for i in range(nx)])  4.12 us
    pallas_call x1, Pallas kernels, last_product(): pl.pallas_call(last_kernel, in_specs=[INSIDE] * 8, out_specs=INSIDE, out_...  3.44 us
  transfers between devices with their start and end apart: 12, of which 5 were waited for; matrix products, arithmetic and copies ran while one was open for 2% of the time, Pallas kernels for 8%

profile of v2, /device:TPU:1, one launch (start us, length us, event | category | flops | bytes accessed | tf_op | source)
XLA Modules:
  0.0 134.1 jit_solution(8458405076043348073)
XLA Ops:
  0.6 0.0 copy-start
  0.6 0.0 copy-start.1
  0.7 8.9 %collective-permute-start.5 = (bf16[512,4608]{1,0:T(8,128)(2,1)}, bf16[512,4608]{1,0:T(8,128)(2,1)}, u32[]{:S(2)}, u32[]{:S(2)}) collective-permute-start(bf16[512,4608]{1,0:T(8,128)(2,1)} %w0.1), channel_id=1, source_target_pairs={{0,64},{64,0},{1,65},{65,1},{2,66},{66,2},{3,67},{67,3},{4,68},{68... | collective-permute-start | bytes 14155784 | tf_op jit(solution)/shard_map/ppermute | solution.py:274
  9.5 1.9 %norm.1 = (bf16[64,2,3584]{2,1,0:T(2,128)(2,1)}, bf16[2,1024]{1,0:T(2,128)(2,1)S(1)}) custom-call(bf16[2,4608]{1,0:T(2,128)(2,1)} %hidden.1, f32[4608]{0:T(1024)} %gain.1), custom_call_target="tpu_custom_call" | custom-call | tf_op jit(solution)/shard_map/norm/pallas_call | solution.py:48
  11.4 11.0 %all-to-all-start = ((bf16[64,2,3584]{2,1,0:T(2,128)(2,1)}), bf16[64,2,3584]{2,1,0:T(2,128)(2,1)S(1)}, u32[]{:S(2)}, u32[]{:S(2)}) async-start(bf16[64,2,3584]{2,1,0:T(2,128)(2,1)} %get-tuple-element.10), calls=%async_computation | async-start | bytes 1835008 | tf_op jit(solution)/shard_map/all_to_all | solution.py:260
  22.4 3.1 %collective-permute-start.2 = (bf16[2,1024]{1,0:T(2,128)(2,1)S(1)}, bf16[2,1024]{1,0:T(2,128)(2,1)S(1)}, u32[]{:S(2)}, u32[]{:S(2)}) collective-permute-start(bf16[2,1024]{1,0:T(2,128)(2,1)S(1)} %get-tuple-element.11), channel_id=1, source_target_pairs={{0,128},{128,256},{256,384},{384,0},{1,129},{129,257},{257,385},{3... | collective-permute-start | bytes 12296 | tf_op jit(solution)/shard_map/ppermute | solution.py:270
  25.5 3.4 %collective-permute-start.3 = (bf16[2,1024]{1,0:T(2,128)(2,1)S(1)}, bf16[2,1024]{1,0:T(2,128)(2,1)S(1)}, u32[]{:S(2)}, u32[]{:S(2)}) collective-permute-start(bf16[2,1024]{1,0:T(2,128)(2,1)S(1)} %get-tuple-element.11), channel_id=1, source_target_pairs={{0,384},{128,0},{256,128},{384,256},{1,385},{129,1},{257,129},{385... | collective-permute-start | bytes 12296 | tf_op jit(solution)/shard_map/ppermute | solution.py:270
  28.9 3.4 %collective-permute-start.4 = (bf16[2,1024]{1,0:T(2,128)(2,1)S(1)}, bf16[2,1024]{1,0:T(2,128)(2,1)S(1)}, u32[]{:S(2)}, u32[]{:S(2)}) collective-permute-start(bf16[2,1024]{1,0:T(2,128)(2,1)S(1)} %get-tuple-element.11), channel_id=1, source_target_pairs={{0,256},{128,384},{256,0},{384,128},{1,257},{129,385},{257,1},{385... | collective-permute-start | bytes 12296 | tf_op jit(solution)/shard_map/ppermute | solution.py:270
  32.4 0.0 collective-permute-done.2
  32.4 0.0 collective-permute-done.3
  32.4 2.7 %collective-permute-done.4 = bf16[2,1024]{1,0:T(2,128)(2,1)S(1)} collective-permute-done((bf16[2,1024]{1,0:T(2,128)(2,1)S(1)}, bf16[2,1024]{1,0:T(2,128)(2,1)S(1)}, u32[]{:S(2)}, u32[]{:S(2)}) %collective-permute-start.4) | collective-permute-done | bytes 4128 | tf_op jit(solution)/shard_map/ppermute | solution.py:270
  35.1 12.7 %all-to-all-done = bf16[64,2,3584]{2,1,0:T(2,128)(2,1)S(1)} async-done(((bf16[64,2,3584]{2,1,0:T(2,128)(2,1)}), bf16[64,2,3584]{2,1,0:T(2,128)(2,1)S(1)}, u32[]{:S(2)}, u32[]{:S(2)}) %all-to-all-start) | async-done | bytes 917536 | tf_op jit(solution)/shard_map/all_to_all | solution.py:260
  47.8 1.1 broadcast_in_dim.2
  49.0 7.5 %all-to-all-start.1 = ((bf16[64,8,1024]{2,1,0:T(8,128)(2,1)}), bf16[64,8,1024]{2,1,0:T(8,128)(2,1)S(1)}, u32[]{:S(2)}, u32[]{:S(2)}) async-start(bf16[64,8,1024]{2,1,0:T(8,128)(2,1)} %broadcast_in_dim.2), calls=%async_computation.1 | async-start | bytes 2097152 | tf_op jit(solution)/shard_map/all_to_all | solution.py:260
  56.5 0.6 fusion
  57.2 0.2 slice.13.x0
  57.3 3.1 %collective-permute-start = (bf16[64,3584]{1,0:T(8,128)(2,1)S(1)}, bf16[64,3584]{1,0:T(8,128)(2,1)S(1)}, u32[]{:S(2)}, u32[]{:S(2)}) collective-permute-start(bf16[64,3584]{1,0:T(8,128)(2,1)S(1)} %slice.13.x0), channel_id=1, source_target_pairs={{0,128},{128,256},{256,384},{384,0},{1,129},{129,257},{257,385},{3... | collective-permute-start | bytes 1376264 | tf_op jit(solution)/shard_map/ppermute | solution.py:270
  60.5 0.2 slice.15.x1
  60.6 3.4 %collective-permute-start.7 = (bf16[64,3584]{1,0:T(8,128)(2,1)S(1)}, bf16[64,3584]{1,0:T(8,128)(2,1)S(1)}, u32[]{:S(2)}, u32[]{:S(2)}) collective-permute-start(bf16[64,3584]{1,0:T(8,128)(2,1)S(1)} %slice.15.x1), channel_id=1, source_target_pairs={{0,384},{128,0},{256,128},{384,256},{1,385},{129,1},{257,129},{385... | collective-permute-start | bytes 1376264 | tf_op jit(solution)/shard_map/ppermute | solution.py:270
  64.0 1.9 %collective-permute-start.1 = (bf16[64,3584]{1,0:T(8,128)(2,1)S(1)}, bf16[64,3584]{1,0:T(8,128)(2,1)}, u32[]{:S(2)}, u32[]{:S(2)}) collective-permute-start(bf16[64,3584]{1,0:T(8,128)(2,1)S(1)} %slice.15.x1), channel_id=1, source_target_pairs={{0,128},{128,256},{256,384},{384,0},{1,129},{129,257},{257,385},{3... | collective-permute-start | bytes 1376264 | tf_op jit(solution)/shard_map/ppermute | solution.py:270
  66.0 4.6 %collective-permute-start.6 = (bf16[64,3584]{1,0:T(8,128)(2,1)S(1)}, bf16[64,3584]{1,0:T(8,128)(2,1)S(1)}, u32[]{:S(2)}, u32[]{:S(2)}) collective-permute-start(bf16[64,3584]{1,0:T(8,128)(2,1)S(1)} %slice.13.x0), channel_id=1, source_target_pairs={{0,384},{128,0},{256,128},{384,256},{1,385},{129,1},{257,129},{385... | collective-permute-start | bytes 1376264 | tf_op jit(solution)/shard_map/ppermute | solution.py:270
  70.5 0.5 collective-permute-done.x2
  71.0 1.9 %collective-permute-start.8 = (bf16[64,3584]{1,0:T(8,128)(2,1)S(1)}, bf16[64,3584]{1,0:T(8,128)(2,1)}, u32[]{:S(2)}, u32[]{:S(2)}) collective-permute-start(bf16[64,3584]{1,0:T(8,128)(2,1)S(1)} %collective-permute-done.x2), channel_id=1, source_target_pairs={{0,128},{128,256},{256,384},{384,0},{1,129},{129,257},{257,385},{3... | collective-permute-start | bytes 1376264 | tf_op jit(solution)/shard_map/ppermute | solution.py:270
  72.9 0.0 collective-permute-done.7.x1
  72.9 4.6 %collective-permute-start.9 = (bf16[64,3584]{1,0:T(8,128)(2,1)S(1)}, bf16[64,3584]{1,0:T(8,128)(2,1)}, u32[]{:S(2)}, u32[]{:S(2)}) collective-permute-start(bf16[64,3584]{1,0:T(8,128)(2,1)S(1)} %collective-permute-done.7.x1), channel_id=1, source_target_pairs={{0,384},{128,0},{256,128},{384,256},{1,385},{129,1},{257,129},{385... | collective-permute-start | bytes 1376264 | tf_op jit(solution)/shard_map/ppermute | solution.py:270
  77.5 5.8 %all-to-all-done.1 = bf16[64,8,1024]{2,1,0:T(8,128)(2,1)S(1)} async-done(((bf16[64,8,1024]{2,1,0:T(8,128)(2,1)}), bf16[64,8,1024]{2,1,0:T(8,128)(2,1)S(1)}, u32[]{:S(2)}, u32[]{:S(2)}) %all-to-all-start.1) | async-done | bytes 1048608 | tf_op jit(solution)/shard_map/all_to_all | solution.py:260
  83.3 0.0 collective-permute-done.1.x3
  83.3 0.0 collective-permute-done.5.w1
  83.3 0.0 copy-done
  83.3 0.0 copy-done.1
  83.4 8.3 %first_product.1 = (f32[1024,256]{1,0:T(8,128)S(1)}, f32[8,128]{1,0:T(8,128)S(1)}, f32[16,128]{1,0:T(8,128)S(1)}, bf16[1024,3584]{1,0:T(8,128)(2,1)S(1)}) custom-call(s32[32]{0:T(128)S(1)} %copy-done.1, s32[8,128]{1,0:T(8,128)S(1)} %bitcast.4, bf16[64,3584]{1,0:T(8,128)(2,1)S(1)} %slice.13.x0, bf16[64,3584]{1,0:T(8,128)(2,1)S(1)} %slice.15.x1, ...), custom_call_target="tpu_custom_call" | custom-call | flops 2415919104 | bytes 14680064 | tf_op jit(solution)/shard_map/first_product/pallas_call | solution.py:162
  91.6 0.0 collective-permute-done.6.x0
  91.6 0.0 collective-permute-done.8.x2
  91.7 0.9 collective-permute-done.9.x3
  92.6 3.4 %last_product.1 = f32[64,8,128]{2,1,0:T(8,128)S(1)} custom-call(s32[8,128]{1,0:T(8,128)S(1)} %bitcast.5, f32[1024,256]{1,0:T(8,128)S(1)} %get-tuple-element.13.late, f32[8,128]{1,0:T(8,128)S(1)} %get-tuple-element.14.early_stat, bf16[64,3584]{1,0:T(8,128)(2,1)S(1)} %collective-permute-done.6.x0, bf16[64,3584]{1,0:T(8,128)(2,1)S(1)} %collective-permute-done.7.x1, ...), custom_call_target="tpu_custom_call" | custom-call | flops 1879048192 | bytes 10485760 | tf_op jit(solution)/shard_map/last_product/pallas_call | solution.py:197
  96.1 24.1 %all_to_all.20.parts = f32[64,8,128]{2,1,0:T(8,128)S(1)} all-to-all(f32[64,8,128]{2,1,0:T(8,128)S(1)} %last_product.1), channel_id=1, replica_groups=mesh['x'=4,'c'=2,'z'=8,'y'=8] {'z','y'}, dimensions={0} | all-to-all | bytes 524288 | tf_op jit(solution)/shard_map/all_to_all | solution.py:260
  120.2 0.1 join.1
  120.3 13.1 %all_to_all.21.parts = f32[8,8,128]{2,1,0:T(8,128)S(1)} all-to-all(f32[8,8,128]{2,1,0:T(8,128)S(1)} %join.1), channel_id=1, replica_groups=mesh['x'=4,'c'=2,'z'=8,'y'=8] {'x','c'}, dimensions={0} | all-to-all | bytes 65536 | tf_op jit(solution)/shard_map/all_to_all | solution.py:260
  133.4 0.7 final_loss.1
  (1 shorter events, 0.0 us)
Async XLA Ops:
  0.6 82.7 %copy-start = (s32[1024]{0:T(1024)S(1)}, s32[1024]{0:T(1024)}, u32[]{:S(2)}) copy-start(s32[1024]{0:T(1024)} %param.8) | copy-start | bytes 12292
  0.6 82.7 %copy-start.1 = (s32[32]{0:T(128)S(1)}, s32[32]{0:T(128)}, u32[]{:S(2)}) copy-start(s32[32]{0:T(128)} %lengths.1) | copy-start | bytes 388
  0.7 82.7 %collective-permute-start.5 = (bf16[512,4608]{1,0:T(8,128)(2,1)}, bf16[512,4608]{1,0:T(8,128)(2,1)}, u32[]{:S(2)}, u32[]{:S(2)}) collective-permute-start(bf16[512,4608]{1,0:T(8,128)(2,1)} %w0.1), channel_id=1, source_target_pairs={{0,64},{64,0},{1,65},{65,1},{2,66},{66,2},{3,67},{67,3},{4,68},{68... | collective-permute-start | bytes 14155784 | tf_op jit(solution)/shard_map/ppermute | solution.py:274
  11.4 36.4 %all-to-all-start = ((bf16[64,2,3584]{2,1,0:T(2,128)(2,1)}), bf16[64,2,3584]{2,1,0:T(2,128)(2,1)S(1)}, u32[]{:S(2)}, u32[]{:S(2)}) async-start(bf16[64,2,3584]{2,1,0:T(2,128)(2,1)} %get-tuple-element.10), calls=%async_computation | async-start | bytes 1835008 | tf_op jit(solution)/shard_map/all_to_all | solution.py:260
  22.4 10.0 %collective-permute-start.2 = (bf16[2,1024]{1,0:T(2,128)(2,1)S(1)}, bf16[2,1024]{1,0:T(2,128)(2,1)S(1)}, u32[]{:S(2)}, u32[]{:S(2)}) collective-permute-start(bf16[2,1024]{1,0:T(2,128)(2,1)S(1)} %get-tuple-element.11), channel_id=1, source_target_pairs={{0,128},{128,256},{256,384},{384,0},{1,129},{129,257},{257,385},{3... | collective-permute-start | bytes 12296 | tf_op jit(solution)/shard_map/ppermute | solution.py:270
  25.5 6.8 %collective-permute-start.3 = (bf16[2,1024]{1,0:T(2,128)(2,1)S(1)}, bf16[2,1024]{1,0:T(2,128)(2,1)S(1)}, u32[]{:S(2)}, u32[]{:S(2)}) collective-permute-start(bf16[2,1024]{1,0:T(2,128)(2,1)S(1)} %get-tuple-element.11), channel_id=1, source_target_pairs={{0,384},{128,0},{256,128},{384,256},{1,385},{129,1},{257,129},{385... | collective-permute-start | bytes 12296 | tf_op jit(solution)/shard_map/ppermute | solution.py:270
  28.9 6.2 %collective-permute-start.4 = (bf16[2,1024]{1,0:T(2,128)(2,1)S(1)}, bf16[2,1024]{1,0:T(2,128)(2,1)S(1)}, u32[]{:S(2)}, u32[]{:S(2)}) collective-permute-start(bf16[2,1024]{1,0:T(2,128)(2,1)S(1)} %get-tuple-element.11), channel_id=1, source_target_pairs={{0,256},{128,384},{256,0},{384,128},{1,257},{129,385},{257,1},{385... | collective-permute-start | bytes 12296 | tf_op jit(solution)/shard_map/ppermute | solution.py:270
  49.0 34.4 %all-to-all-start.1 = ((bf16[64,8,1024]{2,1,0:T(8,128)(2,1)}), bf16[64,8,1024]{2,1,0:T(8,128)(2,1)S(1)}, u32[]{:S(2)}, u32[]{:S(2)}) async-start(bf16[64,8,1024]{2,1,0:T(8,128)(2,1)} %broadcast_in_dim.2), calls=%async_computation.1 | async-start | bytes 2097152 | tf_op jit(solution)/shard_map/all_to_all | solution.py:260
  57.3 13.7 %collective-permute-start = (bf16[64,3584]{1,0:T(8,128)(2,1)S(1)}, bf16[64,3584]{1,0:T(8,128)(2,1)S(1)}, u32[]{:S(2)}, u32[]{:S(2)}) collective-permute-start(bf16[64,3584]{1,0:T(8,128)(2,1)S(1)} %slice.13.x0), channel_id=1, source_target_pairs={{0,128},{128,256},{256,384},{384,0},{1,129},{129,257},{257,385},{3... | collective-permute-start | bytes 1376264 | tf_op jit(solution)/shard_map/ppermute | solution.py:270
  60.6 12.3 %collective-permute-start.7 = (bf16[64,3584]{1,0:T(8,128)(2,1)S(1)}, bf16[64,3584]{1,0:T(8,128)(2,1)S(1)}, u32[]{:S(2)}, u32[]{:S(2)}) collective-permute-start(bf16[64,3584]{1,0:T(8,128)(2,1)S(1)} %slice.15.x1), channel_id=1, source_target_pairs={{0,384},{128,0},{256,128},{384,256},{1,385},{129,1},{257,129},{385... | collective-permute-start | bytes 1376264 | tf_op jit(solution)/shard_map/ppermute | solution.py:270
  64.0 19.3 %collective-permute-start.1 = (bf16[64,3584]{1,0:T(8,128)(2,1)S(1)}, bf16[64,3584]{1,0:T(8,128)(2,1)}, u32[]{:S(2)}, u32[]{:S(2)}) collective-permute-start(bf16[64,3584]{1,0:T(8,128)(2,1)S(1)} %slice.15.x1), channel_id=1, source_target_pairs={{0,128},{128,256},{256,384},{384,0},{1,129},{129,257},{257,385},{3... | collective-permute-start | bytes 1376264 | tf_op jit(solution)/shard_map/ppermute | solution.py:270
  66.0 25.7 %collective-permute-start.6 = (bf16[64,3584]{1,0:T(8,128)(2,1)S(1)}, bf16[64,3584]{1,0:T(8,128)(2,1)S(1)}, u32[]{:S(2)}, u32[]{:S(2)}) collective-permute-start(bf16[64,3584]{1,0:T(8,128)(2,1)S(1)} %slice.13.x0), channel_id=1, source_target_pairs={{0,384},{128,0},{256,128},{384,256},{1,385},{129,1},{257,129},{385... | collective-permute-start | bytes 1376264 | tf_op jit(solution)/shard_map/ppermute | solution.py:270
  71.0 20.6 %collective-permute-start.8 = (bf16[64,3584]{1,0:T(8,128)(2,1)S(1)}, bf16[64,3584]{1,0:T(8,128)(2,1)}, u32[]{:S(2)}, u32[]{:S(2)}) collective-permute-start(bf16[64,3584]{1,0:T(8,128)(2,1)S(1)} %collective-permute-done.x2), channel_id=1, source_target_pairs={{0,128},{128,256},{256,384},{384,0},{1,129},{129,257},{257,385},{3... | collective-permute-start | bytes 1376264 | tf_op jit(solution)/shard_map/ppermute | solution.py:270
  72.9 19.7 %collective-permute-start.9 = (bf16[64,3584]{1,0:T(8,128)(2,1)S(1)}, bf16[64,3584]{1,0:T(8,128)(2,1)}, u32[]{:S(2)}, u32[]{:S(2)}) collective-permute-start(bf16[64,3584]{1,0:T(8,128)(2,1)S(1)} %collective-permute-done.7.x1), channel_id=1, source_target_pairs={{0,384},{128,0},{256,128},{384,256},{1,385},{129,1},{257,129},{385... | collective-permute-start | bytes 1376264 | tf_op jit(solution)/shard_map/ppermute | solution.py:270

commit v3 on v2

--- a/solution.py
+++ b/solution.py
@@ -99,24 +99,12 @@
     return copies
 
 
-def first_kernel(
-    lengths, targets, x0, x1, x2, x3, mixed, w0, w1, late, stat, live, kept, rows, logits, narrow_w, sems
-):
+def early_kernel(lengths, x0, x1, x2, x3, w0, w1, logits, live, weight, sems):
     wide = x0.shape[1]
-    tokens = mixed.shape[0]
-    groups = tokens // 128
-    early = logits.shape[1]
-    half = tokens // 2
-    vocab = w0.shape[0]
-    copies = [
-        pltpu.make_async_copy(w.at[:, wide:], narrow_w.at[j * vocab:(j + 1) * vocab, :], sems.at[2 * CHUNKS + j])
-        for j, w in enumerate((w0, w1))
-    ]
-    for copy in copies:
-        copy.start()
     width = wide // CHUNKS
-    others = fetch((w0, w1), kept, sems, [i * width for i in range(CHUNKS)], width)
+    copies = fetch((w0, w1), weight, sems, [i * width for i in range(CHUNKS)], width)
     lane = lax.broadcasted_iota(jnp.int32, (1, 128), 1)
+    groups = live.shape[0] // 4
     count = 0
     for core in range(2):
         for k in range(groups):
@@ -128,6 +116,55 @@
             i = core * groups + k
             live[i:i + 1, :] = jnp.where(lane % WINDOW < length, 1.0, 0.0)
     live[2 * groups:, :] = jnp.full((2 * groups, 128), count, jnp.int32).astype(jnp.float32)
+    for i in range(CHUNKS):
+        for copy in copies[i]:
+            copy.wait()
+        cols = slice(i * width, (i + 1) * width)
+        x = jnp.concatenate([x0[:, cols], x1[:, cols], x2[:, cols], x3[:, cols]], axis=0)
+        part = dot_t(weight[:, cols], x)
+        if i == 0:
+            logits[...] = part
+        else:
+            logits[...] += part
+
+
+INSIDE = pl.BlockSpec(memory_space=pltpu.VMEM)
+OUTSIDE = pl.BlockSpec(memory_space=pltpu.HBM)
+
+
+def early_product(lengths, xs, w0, w1):
+    vocab = 2 * w0.shape[0]
+    wide = xs[0].shape[1]
+    tokens = sum(x.shape[0] for x in xs)
+    return pl.pallas_call(
+        early_kernel,
+        in_specs=[scalars()] + [INSIDE] * 4 + [OUTSIDE] * 2,
+        out_specs=[INSIDE] * 2,
+        out_shape=[
+            jax.ShapeDtypeStruct((vocab, tokens), jnp.float32),
+            jax.ShapeDtypeStruct((16, 128), jnp.float32),
+        ],
+        scratch_shapes=[pltpu.VMEM((vocab, wide), w0.dtype), pltpu.SemaphoreType.DMA((2 * CHUNKS,))],
+        compiler_params=params(WIDE_VMEM),
+        cost_estimate=pl.CostEstimate(flops=2 * vocab * tokens * wide, bytes_accessed=10 * 2**20, transcendentals=0),
+        name="early_product",
+    )(lengths, *xs, w0, w1)
+
+
+def mixed_kernel(targets, near, mixed, w0, w1, late, stat, kept, rows, logits, narrow_w, sems):
+    tokens = mixed.shape[0]
+    groups = tokens // 128
+    early = logits.shape[1]
+    half = tokens // 2
+    vocab = w0.shape[0]
+    wide = kept.shape[1]
+    copies = [
+        pltpu.make_async_copy(w.at[:, wide:], narrow_w.at[j * vocab:(j + 1) * vocab, :], sems.at[2 + j])
+        for j, w in enumerate((w0, w1))
+    ]
+    for copy in copies:
+        copy.start()
+    others = fetch((w0, w1), kept, sems, [0], wide)
     row = lax.broadcasted_iota(jnp.int32, (half, half), 0)
     col = lax.broadcasted_iota(jnp.int32, (half, half), 1)
     inner = row & 63
@@ -140,45 +177,37 @@
     for copy in copies:
         copy.wait()
     late[...] = dot_t(narrow_w[...], rows[early:, :])
-    logits[...] = dot_t(narrow_w[...], rows[:early, :])
-    for i in range(CHUNKS):
-        for copy in others[i]:
-            copy.wait()
-        cols = slice(i * width, (i + 1) * width)
-        x = jnp.concatenate([x0[:, cols], x1[:, cols], x2[:, cols], x3[:, cols]], axis=0)
-        logits[...] += dot_t(kept[:, cols], x)
+    logits[...] = near[...] + dot_t(narrow_w[...], rows[:early, :])
     for i, total in enumerate(token_sums(targets, (0, 1), logits)):
         for k in range(2):
             stat[2 * i + k:2 * i + k + 1, :] = total[:, k * 128:(k + 1) * 128]
-
-
-INSIDE = pl.BlockSpec(memory_space=pltpu.VMEM)
-
-
-def first_product(lengths, targets, xs, mixed, w0, w1):
+    for copy in others[0]:
+        copy.wait()
+
+
+def mixed_product(targets, near, mixed, w0, w1):
     vocab, depth = 2 * w0.shape[0], w0.shape[1]
     tokens, narrow = mixed.shape
-    early = sum(x.shape[0] for x in xs)
-    return pl.pallas_call(
-        first_kernel,
-        in_specs=[scalars()] + [INSIDE] * 6 + [pl.BlockSpec(memory_space=pltpu.HBM)] * 2,
-        out_specs=[INSIDE] * 4,
+    early = near.shape[1]
+    return pl.pallas_call(
+        mixed_kernel,
+        in_specs=[INSIDE] * 3 + [OUTSIDE] * 2,
+        out_specs=[INSIDE] * 3,
         out_shape=[
             jax.ShapeDtypeStruct((vocab, tokens - early), jnp.float32),
             jax.ShapeDtypeStruct((8, 128), jnp.float32),
-            jax.ShapeDtypeStruct((16, 128), jnp.float32),
             jax.ShapeDtypeStruct((vocab, depth - narrow), w0.dtype),
         ],
         scratch_shapes=[
             pltpu.VMEM((tokens, narrow), jnp.bfloat16),
             pltpu.VMEM((vocab, early), jnp.float32),
             pltpu.VMEM((vocab, narrow), w0.dtype),
-            pltpu.SemaphoreType.DMA((2 * CHUNKS + 2,)),
+            pltpu.SemaphoreType.DMA((4,)),
         ],
         compiler_params=params(WIDE_VMEM),
-        cost_estimate=pl.CostEstimate(flops=vocab * tokens * depth, bytes_accessed=14 * 2**20, transcendentals=0),
-        name="first_product",
-    )(lengths, targets, *xs, mixed, w0, w1)
+        cost_estimate=pl.CostEstimate(flops=2 * vocab * tokens * narrow, bytes_accessed=12 * 2**20, transcendentals=0),
+        name="mixed_product",
+    )(targets, near, mixed, w0, w1)
 
 
 def last_kernel(targets, late, early_stat, x0, x1, x2, x3, weight, out, logits, stat):
@@ -226,9 +255,7 @@
 def loss_kernel(live, parts, token_loss, mean_loss, loss):
     groups = parts.shape[1] // 2
     for core in range(2):
-        total = parts[core]
-        for i in range(core + 2, parts.shape[0], 2):
-            total = total + parts[i]
+        total = jnp.sum(parts[core * parts.shape[0] // 2:(core + 1) * parts.shape[0] // 2], axis=0)
         rows = slice(core * groups, (core + 1) * groups)
         loss[rows, :] = live[rows, :] * (jnp.log(total[:groups]) - total[groups:])
     mean_loss[0] = jnp.sum(loss[...]) / live[2 * groups, 0]
@@ -280,10 +307,11 @@
     far_low, far_high = turn(up_low, 1), turn(down_high, nx - 1)
     ids = targets.reshape(nx * nc, block)
     shards = in_hbm(head_weight), in_hbm(other_weight)
-    late, early, live, wide_w = first_product(lengths, ids, (low, high, up_low, up_high), mixed, *shards)
-    stats = last_product(ids, late, early, (down_low, down_high, far_low, far_high), wide_w, plane)
-    stats = join(exchange(stats, PLANE), nx * nc)
-    stats = exchange(stats, ("x", "c"))
+    near, live = early_product(lengths, (low, high, up_low, up_high), *shards)
+    late, early, wide_w = mixed_product(ids, near, mixed, *shards)
+    stats = last_product(ids, late, early, (down_low, down_high, far_low, far_high), wide_w, lax.axis_size(("x", "z")))
+    stats = join(exchange(stats, ("x", "z")), lax.axis_size(("c", "y")))
+    stats = exchange(stats, ("c", "y"))
     token_loss, mean_loss = final_loss(live, stats, own_rows)
     return (token_loss, mean_loss.reshape(()))
 

time: 135 us -> 134 us (level)
  Pallas kernels: 14.4 us -> 17.5 us
  waiting for transfers between devices: 22.7 us -> 19.6 us
    all_to_all x2, waiting for transfers between devices: 18.5 us -> 12.1 us  [exchange(): return lax.all_to_all(value, axes, 0, 0)]
    ppermute x9, waiting for transfers between devices: 4.12 us -> 7.52 us  [turn(): return lax.ppermute(value, 'x', [(i, (i + k) % nx) for i in range(nx)])]
    pallas_call x1 -> x2, Pallas kernels: 8.27 us -> 11.3 us  [the longest x1 7.27 us: early_product(): pl.pallas_call(early_kernel, in_specs=[scalars()] + [INSIDE] * 4 + [OUTSI...]
  transfers between devices with their start and end apart: 12 -> 12, of which waited for: 5 -> 5; matrix products, arithmetic and copies ran while one was open for 2% -> 2% of each run, Pallas kernels for 8% -> 10%
where the time goes in v3:
time: 134 us; the launch traced here: 133 us
  starting transfers between devices  56.7 us (42%)
  blocking collectives  36.1 us (27%)
  waiting for transfers between devices  19.6 us (15%)
  Pallas kernels  17.5 us (13%)
  local copies, waits for them, and re-layouts  2.12 us (2%)
    all_to_all x2, blocking collectives, exchange(): return lax.all_to_all(value, axes, 0, 0)  36.1 us
    ppermute x9, starting transfers between devices, turn(): return lax.ppermute(value, 'x', [(i, (i + k) % nx) for i in range(nx)])  29.4 us
    all_to_all x2, starting transfers between devices, exchange(): return lax.all_to_all(value, axes, 0, 0)  18.5 us
    all_to_all x2, waiting for transfers between devices, exchange(): return lax.all_to_all(value, axes, 0, 0)  12.1 us
    ppermute x1, starting transfers between devices, body(): other_weight = lax.ppermute(head_weight, 'c', [(0, 1), (1, 0)])  8.75 us
    ppermute x9, waiting for transfers between devices, turn(): return lax.ppermute(value, 'x', [(i, (i + k) % nx) for i in range(nx)])  7.52 us
    pallas_call x1, Pallas kernels, early_product(): pl.pallas_call(early_kernel, in_specs=[scalars()] + [INSIDE] * 4 + [OUTSI...  7.27 us
    pallas_call x1, Pallas kernels, mixed_product(): pl.pallas_call(mixed_kernel, in_specs=[INSIDE] * 3 + [OUTSIDE] * 2, out_s...  4.03 us
  transfers between devices with their start and end apart: 12, of which 5 were waited for; matrix products, arithmetic and copies ran while one was open for 2% of the time, Pallas kernels for 10%

profile of v3, /device:TPU:1, one launch (start us, length us, event | category | flops | bytes accessed | tf_op | source)
XLA Modules:
  0.0 132.9 jit_solution(12307884955237088595)
XLA Ops:
  0.6 0.0 copy-start.1
  0.6 8.8 %collective-permute-start.2 = (bf16[512,4608]{1,0:T(8,128)(2,1)}, bf16[512,4608]{1,0:T(8,128)(2,1)}, u32[]{:S(2)}, u32[]{:S(2)}) collective-permute-start(bf16[512,4608]{1,0:T(8,128)(2,1)} %w0.3), channel_id=1, source_target_pairs={{0,64},{64,0},{1,65},{65,1},{2,66},{66,2},{3,67},{67,3},{4,68},{68... | collective-permute-start | bytes 14155784 | tf_op jit(solution)/shard_map/ppermute | solution.py:301
  9.4 1.9 %norm.1 = (bf16[64,2,3584]{2,1,0:T(2,128)(2,1)}, bf16[2,1024]{1,0:T(2,128)(2,1)S(1)}) custom-call(bf16[2,4608]{1,0:T(2,128)(2,1)} %hidden.1, f32[4608]{0:T(1024)} %gain.1), custom_call_target="tpu_custom_call" | custom-call | tf_op jit(solution)/shard_map/norm/pallas_call | solution.py:48
  11.3 11.0 %all-to-all-start = ((bf16[64,2,3584]{2,1,0:T(2,128)(2,1)}), bf16[64,2,3584]{2,1,0:T(2,128)(2,1)S(1)}, u32[]{:S(2)}, u32[]{:S(2)}) async-start(bf16[64,2,3584]{2,1,0:T(2,128)(2,1)} %get-tuple-element.11), calls=%async_computation | async-start | bytes 1835008 | tf_op jit(solution)/shard_map/all_to_all | solution.py:287
  22.3 4.7 %collective-permute-start.5 = (bf16[2,1024]{1,0:T(2,128)(2,1)S(1)}, bf16[2,1024]{1,0:T(2,128)(2,1)S(1)}, u32[]{:S(2)}, u32[]{:S(2)}) collective-permute-start(bf16[2,1024]{1,0:T(2,128)(2,1)S(1)} %get-tuple-element.14), channel_id=1, source_target_pairs={{0,256},{128,384},{256,0},{384,128},{1,257},{129,385},{257,1},{385... | collective-permute-start | bytes 12296 | tf_op jit(solution)/shard_map/ppermute | solution.py:297
  26.9 2.8 %collective-permute-start.4 = (bf16[2,1024]{1,0:T(2,128)(2,1)S(1)}, bf16[2,1024]{1,0:T(2,128)(2,1)S(1)}, u32[]{:S(2)}, u32[]{:S(2)}) collective-permute-start(bf16[2,1024]{1,0:T(2,128)(2,1)S(1)} %get-tuple-element.14), channel_id=1, source_target_pairs={{0,384},{128,0},{256,128},{384,256},{1,385},{129,1},{257,129},{385... | collective-permute-start | bytes 12296 | tf_op jit(solution)/shard_map/ppermute | solution.py:297
  29.7 2.5 %collective-permute-start.3 = (bf16[2,1024]{1,0:T(2,128)(2,1)S(1)}, bf16[2,1024]{1,0:T(2,128)(2,1)S(1)}, u32[]{:S(2)}, u32[]{:S(2)}) collective-permute-start(bf16[2,1024]{1,0:T(2,128)(2,1)S(1)} %get-tuple-element.14), channel_id=1, source_target_pairs={{0,128},{128,256},{256,384},{384,0},{1,129},{129,257},{257,385},{3... | collective-permute-start | bytes 12296 | tf_op jit(solution)/shard_map/ppermute | solution.py:297
  32.2 0.0 collective-permute-done.5
  32.2 0.0 collective-permute-done.4
  32.3 3.3 %collective-permute-done.3 = bf16[2,1024]{1,0:T(2,128)(2,1)S(1)} collective-permute-done((bf16[2,1024]{1,0:T(2,128)(2,1)S(1)}, bf16[2,1024]{1,0:T(2,128)(2,1)S(1)}, u32[]{:S(2)}, u32[]{:S(2)}) %collective-permute-start.3) | collective-permute-done | bytes 4128 | tf_op jit(solution)/shard_map/ppermute | solution.py:297
  35.6 12.1 %all-to-all-done = bf16[64,2,3584]{2,1,0:T(2,128)(2,1)S(1)} async-done(((bf16[64,2,3584]{2,1,0:T(2,128)(2,1)}), bf16[64,2,3584]{2,1,0:T(2,128)(2,1)S(1)}, u32[]{:S(2)}, u32[]{:S(2)}) %all-to-all-start) | async-done | bytes 917536 | tf_op jit(solution)/shard_map/all_to_all | solution.py:287
  47.7 1.1 broadcast_in_dim.2
  48.8 7.5 %all-to-all-start.1 = ((bf16[64,8,1024]{2,1,0:T(8,128)(2,1)}), bf16[64,8,1024]{2,1,0:T(8,128)(2,1)S(1)}, u32[]{:S(2)}, u32[]{:S(2)}) async-start(bf16[64,8,1024]{2,1,0:T(8,128)(2,1)} %broadcast_in_dim.2), calls=%async_computation.1 | async-start | bytes 2097152 | tf_op jit(solution)/shard_map/all_to_all | solution.py:287
  56.4 0.6 fusion
  57.0 0.2 slice.13.x0
  57.2 3.1 %collective-permute-start = (bf16[64,3584]{1,0:T(8,128)(2,1)S(1)}, bf16[64,3584]{1,0:T(8,128)(2,1)}, u32[]{:S(2)}, u32[]{:S(2)}) collective-permute-start(bf16[64,3584]{1,0:T(8,128)(2,1)S(1)} %slice.13.x0), channel_id=1, source_target_pairs={{0,128},{128,256},{256,384},{384,0},{1,129},{129,257},{257,385},{3... | collective-permute-start | bytes 1376264 | tf_op jit(solution)/shard_map/ppermute | solution.py:297
  60.3 0.2 slice.15.x1
  60.5 0.0 copy-start
  60.5 3.4 %collective-permute-start.7 = (bf16[64,3584]{1,0:T(8,128)(2,1)S(1)}, bf16[64,3584]{1,0:T(8,128)(2,1)S(1)}, u32[]{:S(2)}, u32[]{:S(2)}) collective-permute-start(bf16[64,3584]{1,0:T(8,128)(2,1)S(1)} %slice.15.x1), channel_id=1, source_target_pairs={{0,384},{128,0},{256,128},{384,256},{1,385},{129,1},{257,129},{385... | collective-permute-start | bytes 1376264 | tf_op jit(solution)/shard_map/ppermute | solution.py:297
  63.9 1.9 %collective-permute-start.1 = (bf16[64,3584]{1,0:T(8,128)(2,1)S(1)}, bf16[64,3584]{1,0:T(8,128)(2,1)S(1)}, u32[]{:S(2)}, u32[]{:S(2)}) collective-permute-start(bf16[64,3584]{1,0:T(8,128)(2,1)S(1)} %slice.15.x1), channel_id=1, source_target_pairs={{0,128},{128,256},{256,384},{384,0},{1,129},{129,257},{257,385},{3... | collective-permute-start | bytes 1376264 | tf_op jit(solution)/shard_map/ppermute | solution.py:297
  65.8 4.6 %collective-permute-start.6 = (bf16[64,3584]{1,0:T(8,128)(2,1)S(1)}, bf16[64,3584]{1,0:T(8,128)(2,1)}, u32[]{:S(2)}, u32[]{:S(2)}) collective-permute-start(bf16[64,3584]{1,0:T(8,128)(2,1)S(1)} %slice.13.x0), channel_id=1, source_target_pairs={{0,384},{128,0},{256,128},{384,256},{1,385},{129,1},{257,129},{385... | collective-permute-start | bytes 1376264 | tf_op jit(solution)/shard_map/ppermute | solution.py:297
  70.4 0.6 collective-permute-done.x2
  71.0 1.9 %collective-permute-start.8 = (bf16[64,3584]{1,0:T(8,128)(2,1)}, bf16[64,3584]{1,0:T(8,128)(2,1)}, u32[]{:S(2)}, u32[]{:S(2)}) collective-permute-start(bf16[64,3584]{1,0:T(8,128)(2,1)} %collective-permute-done.x2), channel_id=1, source_target_pairs={{0,128},{128,256},{256,384},{384,0},{1,129},{129,257},{257,385},{3... | collective-permute-start | bytes 1376264 | tf_op jit(solution)/shard_map/ppermute | solution.py:297
  72.9 0.0 collective-permute-done.7.x1
  72.9 4.6 %collective-permute-start.9 = (bf16[64,3584]{1,0:T(8,128)(2,1)S(1)}, bf16[64,3584]{1,0:T(8,128)(2,1)}, u32[]{:S(2)}, u32[]{:S(2)}) collective-permute-start(bf16[64,3584]{1,0:T(8,128)(2,1)S(1)} %collective-permute-done.7.x1), channel_id=1, source_target_pairs={{0,384},{128,0},{256,128},{384,256},{1,385},{129,1},{257,129},{385... | collective-permute-start | bytes 1376264 | tf_op jit(solution)/shard_map/ppermute | solution.py:297
  77.5 3.2 %collective-permute-done.1.x3 = bf16[64,3584]{1,0:T(8,128)(2,1)S(1)} collective-permute-done((bf16[64,3584]{1,0:T(8,128)(2,1)S(1)}, bf16[64,3584]{1,0:T(8,128)(2,1)S(1)}, u32[]{:S(2)}, u32[]{:S(2)}) %collective-permute-start.1) | collective-permute-done | bytes 458784 | tf_op jit(solution)/shard_map/ppermute | solution.py:297
  80.7 0.0 collective-permute-done.2.w1
  80.7 0.0 copy-done.1
  80.7 7.3 %early_product.1 = (f32[1024,256]{1,0:T(8,128)S(1)}, f32[16,128]{1,0:T(8,128)S(1)}) custom-call(s32[32]{0:T(128)S(1)} %copy-done.1, bf16[64,3584]{1,0:T(8,128)(2,1)S(1)} %slice.13.x0, bf16[64,3584]{1,0:T(8,128)(2,1)S(1)} %slice.15.x1, bf16[64,3584]{1,0:T(8,128)(2,1)} %collective-permute-done.x2, bf16[64,3584]{1,0:T(8,128)(2,1)S(1)} %collective-permute-done.1.x3, ...), custom_call_target="tpu_custom_call" | custom-call | flops 1879048192 | bytes 10485760 | tf_op jit(solution)/shard_map/early_product/pallas_call | solution.py:139
  88.0 0.0 all-to-all-done.1
  88.0 0.0 copy-done
  88.0 4.0 %mixed_product.1 = (f32[1024,256]{1,0:T(8,128)S(1)}, f32[8,128]{1,0:T(8,128)S(1)}, bf16[1024,3584]{1,0:T(8,128)(2,1)S(1)}) custom-call(s32[8,128]{1,0:T(8,128)S(1)} %bitcast.4, f32[1024,256]{1,0:T(8,128)S(1)} %get-tuple-element.13.near, bf16[512,1024]{1,0:T(8,128)(2,1)S(1)} %bitcast.3, bf16[512,4608]{1,0:T(8,128)(2,1)} %w0.3, ...), custom_call_target="tpu_custom_call" | custom-call | flops 1073741824 | bytes 12582912 | tf_op jit(solution)/shard_map/mixed_product/pallas_call | solution.py:192
  92.1 0.0 collective-permute-done.6.x0
  92.1 0.0 collective-permute-done.8.x2
  92.1 0.4 collective-permute-done.9.x3
  92.5 3.6 %last_product.1 = f32[32,8,128]{2,1,0:T(8,128)S(1)} custom-call(s32[8,128]{1,0:T(8,128)S(1)} %bitcast.5, f32[1024,256]{1,0:T(8,128)S(1)} %get-tuple-element.15.late, f32[8,128]{1,0:T(8,128)S(1)} %get-tuple-element.16.early_stat, bf16[64,3584]{1,0:T(8,128)(2,1)} %collective-permute-done.6.x0, bf16[64,3584]{1,0:T(8,128)(2,1)S(1)} %collective-permute-done.7.x1, ...), custom_call_target="tpu_custom_call" | custom-call | flops 1879048192 | bytes 10485760 | tf_op jit(solution)/shard_map/last_product/pallas_call | solution.py:226
  96.0 17.8 %all_to_all.20.parts = f32[32,8,128]{2,1,0:T(8,128)S(1)} all-to-all(f32[32,8,128]{2,1,0:T(8,128)S(1)} %last_product.1), channel_id=1, replica_groups=mesh['x'=4,'c'=2,'z'=8,'y'=8] {'x','z'}, dimensions={0} | all-to-all | bytes 262144 | tf_op jit(solution)/shard_map/all_to_all | solution.py:287
  113.8 18.4 %all_to_all.21.parts = f32[16,8,128]{2,1,0:T(8,128)S(1)} all-to-all(f32[16,8,128]{2,1,0:T(8,128)S(1)} %join.1), channel_id=1, replica_groups=mesh['x'=4,'c'=2,'z'=8,'y'=8] {'c','y'}, dimensions={0} | all-to-all | bytes 131072 | tf_op jit(solution)/shard_map/all_to_all | solution.py:287
  132.2 0.7 final_loss.1
  (2 shorter events, 0.1 us)
Async XLA Ops:
  0.6 80.1 %copy-start.1 = (s32[32]{0:T(128)S(1)}, s32[32]{0:T(128)}, u32[]{:S(2)}) copy-start(s32[32]{0:T(128)} %lengths.1) | copy-start | bytes 388
  0.6 80.1 %collective-permute-start.2 = (bf16[512,4608]{1,0:T(8,128)(2,1)}, bf16[512,4608]{1,0:T(8,128)(2,1)}, u32[]{:S(2)}, u32[]{:S(2)}) collective-permute-start(bf16[512,4608]{1,0:T(8,128)(2,1)} %w0.3), channel_id=1, source_target_pairs={{0,64},{64,0},{1,65},{65,1},{2,66},{66,2},{3,67},{67,3},{4,68},{68... | collective-permute-start | bytes 14155784 | tf_op jit(solution)/shard_map/ppermute | solution.py:301
  11.3 36.4 %all-to-all-start = ((bf16[64,2,3584]{2,1,0:T(2,128)(2,1)}), bf16[64,2,3584]{2,1,0:T(2,128)(2,1)S(1)}, u32[]{:S(2)}, u32[]{:S(2)}) async-start(bf16[64,2,3584]{2,1,0:T(2,128)(2,1)} %get-tuple-element.11), calls=%async_computation | async-start | bytes 1835008 | tf_op jit(solution)/shard_map/all_to_all | solution.py:287
  22.3 10.0 %collective-permute-start.5 = (bf16[2,1024]{1,0:T(2,128)(2,1)S(1)}, bf16[2,1024]{1,0:T(2,128)(2,1)S(1)}, u32[]{:S(2)}, u32[]{:S(2)}) collective-permute-start(bf16[2,1024]{1,0:T(2,128)(2,1)S(1)} %get-tuple-element.14), channel_id=1, source_target_pairs={{0,256},{128,384},{256,0},{384,128},{1,257},{129,385},{257,1},{385... | collective-permute-start | bytes 12296 | tf_op jit(solution)/shard_map/ppermute | solution.py:297
  26.9 5.3 %collective-permute-start.4 = (bf16[2,1024]{1,0:T(2,128)(2,1)S(1)}, bf16[2,1024]{1,0:T(2,128)(2,1)S(1)}, u32[]{:S(2)}, u32[]{:S(2)}) collective-permute-start(bf16[2,1024]{1,0:T(2,128)(2,1)S(1)} %get-tuple-element.14), channel_id=1, source_target_pairs={{0,384},{128,0},{256,128},{384,256},{1,385},{129,1},{257,129},{385... | collective-permute-start | bytes 12296 | tf_op jit(solution)/shard_map/ppermute | solution.py:297
  29.7 5.9 %collective-permute-start.3 = (bf16[2,1024]{1,0:T(2,128)(2,1)S(1)}, bf16[2,1024]{1,0:T(2,128)(2,1)S(1)}, u32[]{:S(2)}, u32[]{:S(2)}) collective-permute-start(bf16[2,1024]{1,0:T(2,128)(2,1)S(1)} %get-tuple-element.14), channel_id=1, source_target_pairs={{0,128},{128,256},{256,384},{384,0},{1,129},{129,257},{257,385},{3... | collective-permute-start | bytes 12296 | tf_op jit(solution)/shard_map/ppermute | solution.py:297
  48.8 39.2 %all-to-all-start.1 = ((bf16[64,8,1024]{2,1,0:T(8,128)(2,1)}), bf16[64,8,1024]{2,1,0:T(8,128)(2,1)S(1)}, u32[]{:S(2)}, u32[]{:S(2)}) async-start(bf16[64,8,1024]{2,1,0:T(8,128)(2,1)} %broadcast_in_dim.2), calls=%async_computation.1 | async-start | bytes 2097152 | tf_op jit(solution)/shard_map/all_to_all | solution.py:287
  57.2 13.8 %collective-permute-start = (bf16[64,3584]{1,0:T(8,128)(2,1)S(1)}, bf16[64,3584]{1,0:T(8,128)(2,1)}, u32[]{:S(2)}, u32[]{:S(2)}) collective-permute-start(bf16[64,3584]{1,0:T(8,128)(2,1)S(1)} %slice.13.x0), channel_id=1, source_target_pairs={{0,128},{128,256},{256,384},{384,0},{1,129},{129,257},{257,385},{3... | collective-permute-start | bytes 1376264 | tf_op jit(solution)/shard_map/ppermute | solution.py:297
  60.5 27.5 %copy-start = (s32[1024]{0:T(1024)S(1)}, s32[1024]{0:T(1024)}, u32[]{:S(2)}) copy-start(s32[1024]{0:T(1024)} %param.8) | copy-start | bytes 12292
  60.5 12.4 %collective-permute-start.7 = (bf16[64,3584]{1,0:T(8,128)(2,1)S(1)}, bf16[64,3584]{1,0:T(8,128)(2,1)S(1)}, u32[]{:S(2)}, u32[]{:S(2)}) collective-permute-start(bf16[64,3584]{1,0:T(8,128)(2,1)S(1)} %slice.15.x1), channel_id=1, source_target_pairs={{0,384},{128,0},{256,128},{384,256},{1,385},{129,1},{257,129},{385... | collective-permute-start | bytes 1376264 | tf_op jit(solution)/shard_map/ppermute | solution.py:297
  63.9 16.8 %collective-permute-start.1 = (bf16[64,3584]{1,0:T(8,128)(2,1)S(1)}, bf16[64,3584]{1,0:T(8,128)(2,1)S(1)}, u32[]{:S(2)}, u32[]{:S(2)}) collective-permute-start(bf16[64,3584]{1,0:T(8,128)(2,1)S(1)} %slice.15.x1), channel_id=1, source_target_pairs={{0,128},{128,256},{256,384},{384,0},{1,129},{129,257},{257,385},{3... | collective-permute-start | bytes 1376264 | tf_op jit(solution)/shard_map/ppermute | solution.py:297
  65.8 26.2 %collective-permute-start.6 = (bf16[64,3584]{1,0:T(8,128)(2,1)S(1)}, bf16[64,3584]{1,0:T(8,128)(2,1)}, u32[]{:S(2)}, u32[]{:S(2)}) collective-permute-start(bf16[64,3584]{1,0:T(8,128)(2,1)S(1)} %slice.13.x0), channel_id=1, source_target_pairs={{0,384},{128,0},{256,128},{384,256},{1,385},{129,1},{257,129},{385... | collective-permute-start | bytes 1376264 | tf_op jit(solution)/shard_map/ppermute | solution.py:297
  71.0 21.1 %collective-permute-start.8 = (bf16[64,3584]{1,0:T(8,128)(2,1)}, bf16[64,3584]{1,0:T(8,128)(2,1)}, u32[]{:S(2)}, u32[]{:S(2)}) collective-permute-start(bf16[64,3584]{1,0:T(8,128)(2,1)} %collective-permute-done.x2), channel_id=1, source_target_pairs={{0,128},{128,256},{256,384},{384,0},{1,129},{129,257},{257,385},{3... | collective-permute-start | bytes 1376264 | tf_op jit(solution)/shard_map/ppermute | solution.py:297
  72.9 19.6 %collective-permute-start.9 = (bf16[64,3584]{1,0:T(8,128)(2,1)S(1)}, bf16[64,3584]{1,0:T(8,128)(2,1)}, u32[]{:S(2)}, u32[]{:S(2)}) collective-permute-start(bf16[64,3584]{1,0:T(8,128)(2,1)S(1)} %collective-permute-done.7.x1), channel_id=1, source_target_pairs={{0,384},{128,0},{256,128},{384,256},{1,385},{129,1},{257,129},{385... | collective-permute-start | bytes 1376264 | tf_op jit(solution)/shard_map/ppermute | solution.py:297

commit v4 on v3

--- a/solution.py
+++ b/solution.py
@@ -9,9 +9,8 @@
 WINDOW = 32
 TOK_VOC = ("x", "c", "z", "y")
 PLANE = ("z", "y")
-WIDE = 3584
+WIDE = 3712
 STRIP = 64
-CHUNKS = 2
 VMEM_LIMIT = 12 * 2**20
 WIDE_VMEM = 20 * 2**20
 
@@ -85,14 +84,14 @@
     return jnp.sum(expsum, axis=0, keepdims=True), jnp.sum(picked, axis=0, keepdims=True)
 
 
-def fetch(shards, kept, sems, starts, width):
+def fetch(shards, kept, sems, spans):
     vocab = shards[0].shape[0]
     copies = []
-    for i, start in enumerate(starts):
+    for i, (start, stop) in enumerate(spans):
         pair = []
         for j, shard in enumerate(shards):
-            source = shard.at[:, start:start + width]
-            target = kept.at[j * vocab:(j + 1) * vocab, start:start + width]
+            source = shard.at[:, start:stop]
+            target = kept.at[j * vocab:(j + 1) * vocab, start:stop]
             pair.append(pltpu.make_async_copy(source, target, sems.at[2 * i + j]))
             pair[-1].start()
         copies.append(pair)
@@ -101,8 +100,9 @@
 
 def early_kernel(lengths, x0, x1, x2, x3, w0, w1, logits, live, weight, sems):
     wide = x0.shape[1]
-    width = wide // CHUNKS
-    copies = fetch((w0, w1), weight, sems, [i * width for i in range(CHUNKS)], width)
+    cut = wide // 256 * 128
+    spans = ((0, cut), (cut, wide))
+    copies = fetch((w0, w1), weight, sems, spans)
     lane = lax.broadcasted_iota(jnp.int32, (1, 128), 1)
     groups = live.shape[0] // 4
     count = 0
@@ -116,10 +116,10 @@
             i = core * groups + k
             live[i:i + 1, :] = jnp.where(lane % WINDOW < length, 1.0, 0.0)
     live[2 * groups:, :] = jnp.full((2 * groups, 128), count, jnp.int32).astype(jnp.float32)
-    for i in range(CHUNKS):
+    for i, span in enumerate(spans):
         for copy in copies[i]:
             copy.wait()
-        cols = slice(i * width, (i + 1) * width)
+        cols = slice(*span)
         x = jnp.concatenate([x0[:, cols], x1[:, cols], x2[:, cols], x3[:, cols]], axis=0)
         part = dot_t(weight[:, cols], x)
         if i == 0:
@@ -144,7 +144,7 @@
             jax.ShapeDtypeStruct((vocab, tokens), jnp.float32),
             jax.ShapeDtypeStruct((16, 128), jnp.float32),
         ],
-        scratch_shapes=[pltpu.VMEM((vocab, wide), w0.dtype), pltpu.SemaphoreType.DMA((2 * CHUNKS,))],
+        scratch_shapes=[pltpu.VMEM((vocab, wide), w0.dtype), pltpu.SemaphoreType.DMA((4,))],
         compiler_params=params(WIDE_VMEM),
         cost_estimate=pl.CostEstimate(flops=2 * vocab * tokens * wide, bytes_accessed=10 * 2**20, transcendentals=0),
         name="early_product",
@@ -164,7 +164,7 @@
     ]
     for copy in copies:
         copy.start()
-    others = fetch((w0, w1), kept, sems, [0], wide)
+    others = fetch((w0, w1), kept, sems, ((0, wide),))
     row = lax.broadcasted_iota(jnp.int32, (half, half), 0)
     col = lax.broadcasted_iota(jnp.int32, (half, half), 1)
     inner = row & 63

time: 134 us -> 135 us (level)
  waiting for transfers between devices: 19.6 us -> 21.4 us
where the time goes in v4:
time: 135 us
  starting transfers between devices  56.7 us (42%)
  blocking collectives  35.8 us (27%)
  waiting for transfers between devices  21.4 us (16%)
  Pallas kernels  17.7 us (13%)
  local copies, waits for them, and re-layouts  2.05 us (2%)
    all_to_all x2, blocking collectives, exchange(): return lax.all_to_all(value, axes, 0, 0)  35.8 us
    ppermute x9, starting transfers between devices, turn(): return lax.ppermute(value, 'x', [(i, (i + k) % nx) for i in range(nx)])  29.4 us
    all_to_all x2, starting transfers between devices, exchange(): return lax.all_to_all(value, axes, 0, 0)  18.6 us
    all_to_all x2, waiting for transfers between devices, exchange(): return lax.all_to_all(value, axes, 0, 0)  12.9 us
    ppermute x1, starting transfers between devices, body(): other_weight = lax.ppermute(head_weight, 'c', [(0, 1), (1, 0)])  8.75 us
    ppermute x9, waiting for transfers between devices, turn(): return lax.ppermute(value, 'x', [(i, (i + k) % nx) for i in range(nx)])  8.52 us
    pallas_call x1, Pallas kernels, early_product(): pl.pallas_call(early_kernel, in_specs=[scalars()] + [INSIDE] * 4 + [OUTSI...  7.29 us
    pallas_call x1, Pallas kernels, mixed_product(): pl.pallas_call(mixed_kernel, in_specs=[INSIDE] * 3 + [OUTSIDE] * 2, out_s...  4.03 us
  transfers between devices with their start and end apart: 12, of which 5 were waited for; matrix products, arithmetic and copies ran while one was open for 2% of the time, Pallas kernels for 10%

profile of v4, /device:TPU:1, one launch (start us, length us, event | category | flops | bytes accessed | tf_op | source)
XLA Modules:
  0.0 134.6 jit_solution(6651099777073352173)
XLA Ops:
  0.6 0.0 copy-start.1
  0.6 8.8 %collective-permute-start.2 = (bf16[512,4608]{1,0:T(8,128)(2,1)}, bf16[512,4608]{1,0:T(8,128)(2,1)}, u32[]{:S(2)}, u32[]{:S(2)}) collective-permute-start(bf16[512,4608]{1,0:T(8,128)(2,1)} %w0.3), channel_id=1, source_target_pairs={{0,64},{64,0},{1,65},{65,1},{2,66},{66,2},{3,67},{67,3},{4,68},{68... | collective-permute-start | bytes 14155784 | tf_op jit(solution)/shard_map/ppermute | solution.py:301
  9.4 1.9 %norm.1 = (bf16[64,2,3712]{2,1,0:T(2,128)(2,1)}, bf16[2,896]{1,0:T(2,128)(2,1)S(1)}) custom-call(bf16[2,4608]{1,0:T(2,128)(2,1)} %hidden.1, f32[4608]{0:T(1024)} %gain.1), custom_call_target="tpu_custom_call" | custom-call | tf_op jit(solution)/shard_map/norm/pallas_call | solution.py:47
  11.3 11.0 %all-to-all-start = ((bf16[64,2,3712]{2,1,0:T(2,128)(2,1)}), bf16[64,2,3712]{2,1,0:T(2,128)(2,1)S(1)}, u32[]{:S(2)}, u32[]{:S(2)}) async-start(bf16[64,2,3712]{2,1,0:T(2,128)(2,1)} %get-tuple-element.11), calls=%async_computation | async-start | bytes 1900544 | tf_op jit(solution)/shard_map/all_to_all | solution.py:287
  22.3 4.7 %collective-permute-start.5 = (bf16[2,896]{1,0:T(2,128)(2,1)S(1)}, bf16[2,896]{1,0:T(2,128)(2,1)S(1)}, u32[]{:S(2)}, u32[]{:S(2)}) collective-permute-start(bf16[2,896]{1,0:T(2,128)(2,1)S(1)} %get-tuple-element.14), channel_id=1, source_target_pairs={{0,256},{128,384},{256,0},{384,128},{1,257},{129,385},{257,1},{385... | collective-permute-start | bytes 10760 | tf_op jit(solution)/shard_map/ppermute | solution.py:297
  26.9 2.8 %collective-permute-start.4 = (bf16[2,896]{1,0:T(2,128)(2,1)S(1)}, bf16[2,896]{1,0:T(2,128)(2,1)S(1)}, u32[]{:S(2)}, u32[]{:S(2)}) collective-permute-start(bf16[2,896]{1,0:T(2,128)(2,1)S(1)} %get-tuple-element.14), channel_id=1, source_target_pairs={{0,384},{128,0},{256,128},{384,256},{1,385},{129,1},{257,129},{385... | collective-permute-start | bytes 10760 | tf_op jit(solution)/shard_map/ppermute | solution.py:297
  29.7 2.5 %collective-permute-start.3 = (bf16[2,896]{1,0:T(2,128)(2,1)S(1)}, bf16[2,896]{1,0:T(2,128)(2,1)S(1)}, u32[]{:S(2)}, u32[]{:S(2)}) collective-permute-start(bf16[2,896]{1,0:T(2,128)(2,1)S(1)} %get-tuple-element.14), channel_id=1, source_target_pairs={{0,128},{128,256},{256,384},{384,0},{1,129},{129,257},{257,385},{3... | collective-permute-start | bytes 10760 | tf_op jit(solution)/shard_map/ppermute | solution.py:297
  32.2 0.0 collective-permute-done.5
  32.2 0.0 collective-permute-done.4
  32.3 3.3 %collective-permute-done.3 = bf16[2,896]{1,0:T(2,128)(2,1)S(1)} collective-permute-done((bf16[2,896]{1,0:T(2,128)(2,1)S(1)}, bf16[2,896]{1,0:T(2,128)(2,1)S(1)}, u32[]{:S(2)}, u32[]{:S(2)}) %collective-permute-start.3) | collective-permute-done | bytes 3616 | tf_op jit(solution)/shard_map/ppermute | solution.py:297
  35.6 12.9 %all-to-all-done = bf16[64,2,3712]{2,1,0:T(2,128)(2,1)S(1)} async-done(((bf16[64,2,3712]{2,1,0:T(2,128)(2,1)}), bf16[64,2,3712]{2,1,0:T(2,128)(2,1)S(1)}, u32[]{:S(2)}, u32[]{:S(2)}) %all-to-all-start) | async-done | bytes 950304 | tf_op jit(solution)/shard_map/all_to_all | solution.py:287
  48.5 1.0 broadcast_in_dim.2
  49.5 7.6 %all-to-all-start.1 = ((bf16[64,8,896]{2,1,0:T(8,128)(2,1)}), bf16[64,8,896]{2,1,0:T(8,128)(2,1)S(1)}, u32[]{:S(2)}, u32[]{:S(2)}) async-start(bf16[64,8,896]{2,1,0:T(8,128)(2,1)} %broadcast_in_dim.2), calls=%async_computation.1 | async-start | bytes 1835008 | tf_op jit(solution)/shard_map/all_to_all | solution.py:287
  57.1 0.7 fusion
  57.8 0.2 slice.13.x0
  58.0 3.1 %collective-permute-start = (bf16[64,3712]{1,0:T(8,128)(2,1)S(1)}, bf16[64,3712]{1,0:T(8,128)(2,1)}, u32[]{:S(2)}, u32[]{:S(2)}) collective-permute-start(bf16[64,3712]{1,0:T(8,128)(2,1)S(1)} %slice.13.x0), channel_id=1, source_target_pairs={{0,128},{128,256},{256,384},{384,0},{1,129},{129,257},{257,385},{3... | collective-permute-start | bytes 1425416 | tf_op jit(solution)/shard_map/ppermute | solution.py:297
  61.1 0.2 slice.15.x1
  61.3 0.0 copy-start
  61.3 3.4 %collective-permute-start.7 = (bf16[64,3712]{1,0:T(8,128)(2,1)S(1)}, bf16[64,3712]{1,0:T(8,128)(2,1)S(1)}, u32[]{:S(2)}, u32[]{:S(2)}) collective-permute-start(bf16[64,3712]{1,0:T(8,128)(2,1)S(1)} %slice.15.x1), channel_id=1, source_target_pairs={{0,384},{128,0},{256,128},{384,256},{1,385},{129,1},{257,129},{385... | collective-permute-start | bytes 1425416 | tf_op jit(solution)/shard_map/ppermute | solution.py:297
  64.7 1.9 %collective-permute-start.1 = (bf16[64,3712]{1,0:T(8,128)(2,1)S(1)}, bf16[64,3712]{1,0:T(8,128)(2,1)S(1)}, u32[]{:S(2)}, u32[]{:S(2)}) collective-permute-start(bf16[64,3712]{1,0:T(8,128)(2,1)S(1)} %slice.15.x1), channel_id=1, source_target_pairs={{0,128},{128,256},{256,384},{384,0},{1,129},{129,257},{257,385},{3... | collective-permute-start | bytes 1425416 | tf_op jit(solution)/shard_map/ppermute | solution.py:297
  66.6 4.6 %collective-permute-start.6 = (bf16[64,3712]{1,0:T(8,128)(2,1)S(1)}, bf16[64,3712]{1,0:T(8,128)(2,1)}, u32[]{:S(2)}, u32[]{:S(2)}) collective-permute-start(bf16[64,3712]{1,0:T(8,128)(2,1)S(1)} %slice.13.x0), channel_id=1, source_target_pairs={{0,384},{128,0},{256,128},{384,256},{1,385},{129,1},{257,129},{385... | collective-permute-start | bytes 1425416 | tf_op jit(solution)/shard_map/ppermute | solution.py:297
  71.2 0.9 collective-permute-done.x2
  72.1 1.9 %collective-permute-start.8 = (bf16[64,3712]{1,0:T(8,128)(2,1)}, bf16[64,3712]{1,0:T(8,128)(2,1)}, u32[]{:S(2)}, u32[]{:S(2)}) collective-permute-start(bf16[64,3712]{1,0:T(8,128)(2,1)} %collective-permute-done.x2), channel_id=1, source_target_pairs={{0,128},{128,256},{256,384},{384,0},{1,129},{129,257},{257,385},{3... | collective-permute-start | bytes 1425416 | tf_op jit(solution)/shard_map/ppermute | solution.py:297
  74.0 0.0 collective-permute-done.7.x1
  74.0 4.6 %collective-permute-start.9 = (bf16[64,3712]{1,0:T(8,128)(2,1)S(1)}, bf16[64,3712]{1,0:T(8,128)(2,1)}, u32[]{:S(2)}, u32[]{:S(2)}) collective-permute-start(bf16[64,3712]{1,0:T(8,128)(2,1)S(1)} %collective-permute-done.7.x1), channel_id=1, source_target_pairs={{0,384},{128,0},{256,128},{384,256},{1,385},{129,1},{257,129},{385... | collective-permute-start | bytes 1425416 | tf_op jit(solution)/shard_map/ppermute | solution.py:297
  78.6 3.6 %collective-permute-done.1.x3 = bf16[64,3712]{1,0:T(8,128)(2,1)S(1)} collective-permute-done((bf16[64,3712]{1,0:T(8,128)(2,1)S(1)}, bf16[64,3712]{1,0:T(8,128)(2,1)S(1)}, u32[]{:S(2)}, u32[]{:S(2)}) %collective-permute-start.1) | collective-permute-done | bytes 475168 | tf_op jit(solution)/shard_map/ppermute | solution.py:297
  82.2 0.0 collective-permute-done.2.w1
  82.2 0.0 copy-done.1
  82.2 7.3 %early_product.1 = (f32[1024,256]{1,0:T(8,128)S(1)}, f32[16,128]{1,0:T(8,128)S(1)}) custom-call(s32[32]{0:T(128)S(1)} %copy-done.1, bf16[64,3712]{1,0:T(8,128)(2,1)S(1)} %slice.13.x0, bf16[64,3712]{1,0:T(8,128)(2,1)S(1)} %slice.15.x1, bf16[64,3712]{1,0:T(8,128)(2,1)} %collective-permute-done.x2, bf16[64,3712]{1,0:T(8,128)(2,1)S(1)} %collective-permute-done.1.x3, ...), custom_call_target="tpu_custom_call" | custom-call | flops 1946157056 | bytes 10485760 | tf_op jit(solution)/shard_map/early_product/pallas_call | solution.py:139
  89.5 0.0 all-to-all-done.1
  89.5 0.0 copy-done
  89.5 4.0 %mixed_product.1 = (f32[1024,256]{1,0:T(8,128)S(1)}, f32[8,128]{1,0:T(8,128)S(1)}, bf16[1024,3712]{1,0:T(8,128)(2,1)S(1)}) custom-call(s32[8,128]{1,0:T(8,128)S(1)} %bitcast.4, f32[1024,256]{1,0:T(8,128)S(1)} %get-tuple-element.13.near, bf16[512,896]{1,0:T(8,128)(2,1)S(1)} %bitcast.3, bf16[512,4608]{1,0:T(8,128)(2,1)} %w0.3, ...), custom_call_target="tpu_custom_call" | custom-call | flops 939524096 | bytes 12582912 | tf_op jit(solution)/shard_map/mixed_product/pallas_call | solution.py:192
  93.5 0.0 collective-permute-done.6.x0
  93.5 0.0 collective-permute-done.8.x2
  93.5 0.7 collective-permute-done.9.x3
  94.3 3.7 %last_product.1 = f32[32,8,128]{2,1,0:T(8,128)S(1)} custom-call(s32[8,128]{1,0:T(8,128)S(1)} %bitcast.5, f32[1024,256]{1,0:T(8,128)S(1)} %get-tuple-element.15.late, f32[8,128]{1,0:T(8,128)S(1)} %get-tuple-element.16.early_stat, bf16[64,3712]{1,0:T(8,128)(2,1)} %collective-permute-done.6.x0, bf16[64,3712]{1,0:T(8,128)(2,1)S(1)} %collective-permute-done.7.x1, ...), custom_call_target="tpu_custom_call" | custom-call | flops 1946157056 | bytes 10485760 | tf_op jit(solution)/shard_map/last_product/pallas_call | solution.py:226
  98.0 17.7 %all_to_all.20.parts = f32[32,8,128]{2,1,0:T(8,128)S(1)} all-to-all(f32[32,8,128]{2,1,0:T(8,128)S(1)} %last_product.1), channel_id=1, replica_groups=mesh['x'=4,'c'=2,'z'=8,'y'=8] {'x','z'}, dimensions={0} | all-to-all | bytes 262144 | tf_op jit(solution)/shard_map/all_to_all | solution.py:287
  115.8 18.1 %all_to_all.21.parts = f32[16,8,128]{2,1,0:T(8,128)S(1)} all-to-all(f32[16,8,128]{2,1,0:T(8,128)S(1)} %join.1), channel_id=1, replica_groups=mesh['x'=4,'c'=2,'z'=8,'y'=8] {'c','y'}, dimensions={0} | all-to-all | bytes 131072 | tf_op jit(solution)/shard_map/all_to_all | solution.py:287
  133.9 0.7 final_loss.1
  (2 shorter events, 0.1 us)
Async XLA Ops:
  0.6 81.5 %copy-start.1 = (s32[32]{0:T(128)S(1)}, s32[32]{0:T(128)}, u32[]{:S(2)}) copy-start(s32[32]{0:T(128)} %lengths.1) | copy-start | bytes 388
  0.6 81.5 %collective-permute-start.2 = (bf16[512,4608]{1,0:T(8,128)(2,1)}, bf16[512,4608]{1,0:T(8,128)(2,1)}, u32[]{:S(2)}, u32[]{:S(2)}) collective-permute-start(bf16[512,4608]{1,0:T(8,128)(2,1)} %w0.3), channel_id=1, source_target_pairs={{0,64},{64,0},{1,65},{65,1},{2,66},{66,2},{3,67},{67,3},{4,68},{68... | collective-permute-start | bytes 14155784 | tf_op jit(solution)/shard_map/ppermute | solution.py:301
  11.3 37.2 %all-to-all-start = ((bf16[64,2,3712]{2,1,0:T(2,128)(2,1)}), bf16[64,2,3712]{2,1,0:T(2,128)(2,1)S(1)}, u32[]{:S(2)}, u32[]{:S(2)}) async-start(bf16[64,2,3712]{2,1,0:T(2,128)(2,1)} %get-tuple-element.11), calls=%async_computation | async-start | bytes 1900544 | tf_op jit(solution)/shard_map/all_to_all | solution.py:287
  22.3 10.0 %collective-permute-start.5 = (bf16[2,896]{1,0:T(2,128)(2,1)S(1)}, bf16[2,896]{1,0:T(2,128)(2,1)S(1)}, u32[]{:S(2)}, u32[]{:S(2)}) collective-permute-start(bf16[2,896]{1,0:T(2,128)(2,1)S(1)} %get-tuple-element.14), channel_id=1, source_target_pairs={{0,256},{128,384},{256,0},{384,128},{1,257},{129,385},{257,1},{385... | collective-permute-start | bytes 10760 | tf_op jit(solution)/shard_map/ppermute | solution.py:297
  26.9 5.3 %collective-permute-start.4 = (bf16[2,896]{1,0:T(2,128)(2,1)S(1)}, bf16[2,896]{1,0:T(2,128)(2,1)S(1)}, u32[]{:S(2)}, u32[]{:S(2)}) collective-permute-start(bf16[2,896]{1,0:T(2,128)(2,1)S(1)} %get-tuple-element.14), channel_id=1, source_target_pairs={{0,384},{128,0},{256,128},{384,256},{1,385},{129,1},{257,129},{385... | collective-permute-start | bytes 10760 | tf_op jit(solution)/shard_map/ppermute | solution.py:297
  29.7 5.9 %collective-permute-start.3 = (bf16[2,896]{1,0:T(2,128)(2,1)S(1)}, bf16[2,896]{1,0:T(2,128)(2,1)S(1)}, u32[]{:S(2)}, u32[]{:S(2)}) collective-permute-start(bf16[2,896]{1,0:T(2,128)(2,1)S(1)} %get-tuple-element.14), channel_id=1, source_target_pairs={{0,128},{128,256},{256,384},{384,0},{1,129},{129,257},{257,385},{3... | collective-permute-start | bytes 10760 | tf_op jit(solution)/shard_map/ppermute | solution.py:297
  49.5 40.0 %all-to-all-start.1 = ((bf16[64,8,896]{2,1,0:T(8,128)(2,1)}), bf16[64,8,896]{2,1,0:T(8,128)(2,1)S(1)}, u32[]{:S(2)}, u32[]{:S(2)}) async-start(bf16[64,8,896]{2,1,0:T(8,128)(2,1)} %broadcast_in_dim.2), calls=%async_computation.1 | async-start | bytes 1835008 | tf_op jit(solution)/shard_map/all_to_all | solution.py:287
  58.0 14.1 %collective-permute-start = (bf16[64,3712]{1,0:T(8,128)(2,1)S(1)}, bf16[64,3712]{1,0:T(8,128)(2,1)}, u32[]{:S(2)}, u32[]{:S(2)}) collective-permute-start(bf16[64,3712]{1,0:T(8,128)(2,1)S(1)} %slice.13.x0), channel_id=1, source_target_pairs={{0,128},{128,256},{256,384},{384,0},{1,129},{129,257},{257,385},{3... | collective-permute-start | bytes 1425416 | tf_op jit(solution)/shard_map/ppermute | solution.py:297
  61.3 28.2 %copy-start = (s32[1024]{0:T(1024)S(1)}, s32[1024]{0:T(1024)}, u32[]{:S(2)}) copy-start(s32[1024]{0:T(1024)} %param.8) | copy-start | bytes 12292
  61.3 12.7 %collective-permute-start.7 = (bf16[64,3712]{1,0:T(8,128)(2,1)S(1)}, bf16[64,3712]{1,0:T(8,128)(2,1)S(1)}, u32[]{:S(2)}, u32[]{:S(2)}) collective-permute-start(bf16[64,3712]{1,0:T(8,128)(2,1)S(1)} %slice.15.x1), channel_id=1, source_target_pairs={{0,384},{128,0},{256,128},{384,256},{1,385},{129,1},{257,129},{385... | collective-permute-start | bytes 1425416 | tf_op jit(solution)/shard_map/ppermute | solution.py:297
  64.7 17.5 %collective-permute-start.1 = (bf16[64,3712]{1,0:T(8,128)(2,1)S(1)}, bf16[64,3712]{1,0:T(8,128)(2,1)S(1)}, u32[]{:S(2)}, u32[]{:S(2)}) collective-permute-start(bf16[64,3712]{1,0:T(8,128)(2,1)S(1)} %slice.15.x1), channel_id=1, source_target_pairs={{0,128},{128,256},{256,384},{384,0},{1,129},{129,257},{257,385},{3... | collective-permute-start | bytes 1425416 | tf_op jit(solution)/shard_map/ppermute | solution.py:297
  66.6 26.9 %collective-permute-start.6 = (bf16[64,3712]{1,0:T(8,128)(2,1)S(1)}, bf16[64,3712]{1,0:T(8,128)(2,1)}, u32[]{:S(2)}, u32[]{:S(2)}) collective-permute-start(bf16[64,3712]{1,0:T(8,128)(2,1)S(1)} %slice.13.x0), channel_id=1, source_target_pairs={{0,384},{128,0},{256,128},{384,256},{1,385},{129,1},{257,129},{385... | collective-permute-start | bytes 1425416 | tf_op jit(solution)/shard_map/ppermute | solution.py:297
  72.1 21.5 %collective-permute-start.8 = (bf16[64,3712]{1,0:T(8,128)(2,1)}, bf16[64,3712]{1,0:T(8,128)(2,1)}, u32[]{:S(2)}, u32[]{:S(2)}) collective-permute-start(bf16[64,3712]{1,0:T(8,128)(2,1)} %collective-permute-done.x2), channel_id=1, source_target_pairs={{0,128},{128,256},{256,384},{384,0},{1,129},{129,257},{257,385},{3... | collective-permute-start | bytes 1425416 | tf_op jit(solution)/shard_map/ppermute | solution.py:297
  74.0 20.3 %collective-permute-start.9 = (bf16[64,3712]{1,0:T(8,128)(2,1)S(1)}, bf16[64,3712]{1,0:T(8,128)(2,1)}, u32[]{:S(2)}, u32[]{:S(2)}) collective-permute-start(bf16[64,3712]{1,0:T(8,128)(2,1)S(1)} %collective-permute-done.7.x1), channel_id=1, source_target_pairs={{0,384},{128,0},{256,128},{384,256},{1,385},{129,1},{257,129},{385... | collective-permute-start | bytes 1425416 | tf_op jit(solution)/shard_map/ppermute | solution.py:297

commit v5 on v4

--- a/solution.py
+++ b/solution.py
@@ -9,8 +9,9 @@
 WINDOW = 32
 TOK_VOC = ("x", "c", "z", "y")
 PLANE = ("z", "y")
-WIDE = 3712
+WIDE = 3840
 STRIP = 64
+SEGMENTS = ((0, 0), (0, 1), (1, 0), (2, 1), (2, 0), (1, 1), (3, 0), (3, 1))
 VMEM_LIMIT = 12 * 2**20
 WIDE_VMEM = 20 * 2**20
 
@@ -65,13 +66,19 @@
     return [lax.rem(x + nx - k, nx) for k in (0, 1, nx - 1, 2)]
 
 
-def token_sums(targets, groups, logits):
+def halves(one, two):
+    lane = lax.broadcasted_iota(jnp.int32, one.shape, 1)
+    return jnp.where(lane < 64, one, two)
+
+
+def token_sums(targets, early, logits):
     vocab, tokens = logits.shape
     shard = vocab // 2
     x, c, seat = position(1)
     nc, plane = lax.axis_size("c"), lax.axis_size(PLANE)
     starts = [((x * nc + core) * plane + seat) * shard for core in (c, 1 - c)]
-    wanted = jnp.concatenate([targets[pl.ds(sources(x)[k] * nc + c, 1), :] for k in groups], axis=1)
+    own, up, down, far = [targets[pl.ds(source * nc + c, 1), :] for source in sources(x)]
+    wanted = jnp.concatenate([own, halves(up, down)] if early else [halves(down, up), far], axis=1)
     expsum = jnp.zeros((8, tokens), jnp.float32)
     picked = jnp.zeros((8, tokens), jnp.float32)
     column = lax.broadcasted_iota(jnp.int32, (STRIP, tokens), 0)
@@ -173,12 +180,13 @@
     for h in range(2):
         part = jnp.dot(chosen, mixed[h * half:(h + 1) * half, :], preferred_element_type=jnp.float32)
         for k in range(groups):
-            rows[k * 128 + h * 64:k * 128 + h * 64 + 64, :] = part[k * 64:(k + 1) * 64].astype(jnp.bfloat16)
+            place = SEGMENTS.index((k, h)) * 64
+            rows[place:place + 64, :] = part[k * 64:(k + 1) * 64].astype(jnp.bfloat16)
     for copy in copies:
         copy.wait()
     late[...] = dot_t(narrow_w[...], rows[early:, :])
     logits[...] = near[...] + dot_t(narrow_w[...], rows[:early, :])
-    for i, total in enumerate(token_sums(targets, (0, 1), logits)):
+    for i, total in enumerate(token_sums(targets, True, logits)):
         for k in range(2):
             stat[2 * i + k:2 * i + k + 1, :] = total[:, k * 128:(k + 1) * 128]
     for copy in others[0]:
@@ -213,10 +221,11 @@
 def last_kernel(targets, late, early_stat, x0, x1, x2, x3, weight, out, logits, stat):
     logits[...] = late[...] + dot_t(weight[...], jnp.concatenate([x0[...], x1[...], x2[...], x3[...]], axis=0))
     origin = sources(lax.axis_index("x"))
-    for i, total in enumerate(token_sums(targets, (2, 3), logits)):
-        for k in range(2):
-            stat[pl.ds(origin[k] + 4 * i, 1), :] = early_stat[2 * i + k:2 * i + k + 1, :]
-            stat[pl.ds(origin[2 + k] + 4 * i, 1), :] = total[:, k * 128:(k + 1) * 128]
+    for i, total in enumerate(token_sums(targets, False, logits)):
+        own, soon = early_stat[2 * i:2 * i + 1, :], early_stat[2 * i + 1:2 * i + 2, :]
+        late_part, far = total[:, :128], total[:, 128:]
+        for k, row in enumerate((own, halves(soon, late_part), halves(late_part, soon), far)):
+            stat[pl.ds(origin[k] + 4 * i, 1), :] = row
     for i in range(out.shape[0]):
         out[i] = stat[...]
 
@@ -307,9 +316,9 @@
     far_low, far_high = turn(up_low, 1), turn(down_high, nx - 1)
     ids = targets.reshape(nx * nc, block)
     shards = in_hbm(head_weight), in_hbm(other_weight)
-    near, live = early_product(lengths, (low, high, up_low, up_high), *shards)
+    near, live = early_product(lengths, (low, high, up_low, down_high), *shards)
     late, early, wide_w = mixed_product(ids, near, mixed, *shards)
-    stats = last_product(ids, late, early, (down_low, down_high, far_low, far_high), wide_w, lax.axis_size(("x", "z")))
+    stats = last_product(ids, late, early, (down_low, up_high, far_low, far_high), wide_w, lax.axis_size(("x", "z")))
     stats = join(exchange(stats, ("x", "z")), lax.axis_size(("c", "y")))
     stats = exchange(stats, ("c", "y"))
     token_loss, mean_loss = final_loss(live, stats, own_rows)

time: 135 us -> 137 us (1.015)
  waiting for transfers between devices: 21.4 us -> 24.3 us
    ppermute x9, waiting for transfers between devices: 8.52 us -> 10.7 us  [turn(): return lax.ppermute(value, 'x', [(i, (i + k) % nx) for i in range(nx)])]
  transfers between devices with their start and end apart: 12 -> 12, of which waited for: 5 -> 5; matrix products, arithmetic and copies ran while one was open for 2% -> 1% of each run, Pallas kernels for 10% -> 10%
where the time goes in v5:
time: 137 us
  starting transfers between devices  55.6 us (41%)
  blocking collectives  35.8 us (26%)
  waiting for transfers between devices  24.3 us (18%)
  Pallas kernels  17.9 us (13%)
  local copies, waits for them, and re-layouts  2.01 us (1%)
    all_to_all x2, blocking collectives, exchange(): return lax.all_to_all(value, axes, 0, 0)  35.8 us
    ppermute x9, starting transfers between devices, turn(): return lax.ppermute(value, 'x', [(i, (i + k) % nx) for i in range(nx)])  28.2 us
    all_to_all x2, starting transfers between devices, exchange(): return lax.all_to_all(value, axes, 0, 0)  18.7 us
    all_to_all x2, waiting for transfers between devices, exchange(): return lax.all_to_all(value, axes, 0, 0)  13.6 us
    ppermute x9, waiting for transfers between devices, turn(): return lax.ppermute(value, 'x', [(i, (i + k) % nx) for i in range(nx)])  10.7 us
    ppermute x1, starting transfers between devices, body(): other_weight = lax.ppermute(head_weight, 'c', [(0, 1), (1, 0)])  8.75 us
    pallas_call x1, Pallas kernels, early_product(): pl.pallas_call(early_kernel, in_specs=[scalars()] + [INSIDE] * 4 + [OUTSI...  7.41 us
    pallas_call x1, Pallas kernels, mixed_product(): pl.pallas_call(mixed_kernel, in_specs=[INSIDE] * 3 + [OUTSIDE] * 2, out_s...  3.96 us
  transfers between devices with their start and end apart: 12, of which 5 were waited for; matrix products, arithmetic and copies ran while one was open for 1% of the time, Pallas kernels for 10%

profile of v5, /device:TPU:1, one launch (start us, length us, event | category | flops | bytes accessed | tf_op | source)
XLA Modules:
  0.0 136.5 jit_solution(18226300778922741200)
XLA Ops:
  0.6 0.0 copy-start.1
  0.6 8.8 %collective-permute-start.2 = (bf16[512,4608]{1,0:T(8,128)(2,1)}, bf16[512,4608]{1,0:T(8,128)(2,1)}, u32[]{:S(2)}, u32[]{:S(2)}) collective-permute-start(bf16[512,4608]{1,0:T(8,128)(2,1)} %w0.3), channel_id=1, source_target_pairs={{0,64},{64,0},{1,65},{65,1},{2,66},{66,2},{3,67},{67,3},{4,68},{68... | collective-permute-start | bytes 14155784 | tf_op jit(solution)/shard_map/ppermute | solution.py:310
  9.4 1.9 %norm.1 = (bf16[64,2,3840]{2,1,0:T(2,128)(2,1)}, bf16[2,768]{1,0:T(2,128)(2,1)S(1)}) custom-call(bf16[2,4608]{1,0:T(2,128)(2,1)} %hidden.1, f32[4608]{0:T(1024)} %gain.1), custom_call_target="tpu_custom_call" | custom-call | tf_op jit(solution)/shard_map/norm/pallas_call | solution.py:48
  11.3 11.0 %all-to-all-start = ((bf16[64,2,3840]{2,1,0:T(2,128)(2,1)}), bf16[64,2,3840]{2,1,0:T(2,128)(2,1)S(1)}, u32[]{:S(2)}, u32[]{:S(2)}) async-start(bf16[64,2,3840]{2,1,0:T(2,128)(2,1)} %get-tuple-element.11), calls=%async_computation | async-start | bytes 1966080 | tf_op jit(solution)/shard_map/all_to_all | solution.py:296
  22.3 4.7 %collective-permute-start.5 = (bf16[2,768]{1,0:T(2,128)(2,1)S(1)}, bf16[2,768]{1,0:T(2,128)(2,1)S(1)}, u32[]{:S(2)}, u32[]{:S(2)}) collective-permute-start(bf16[2,768]{1,0:T(2,128)(2,1)S(1)} %get-tuple-element.14), channel_id=1, source_target_pairs={{0,256},{128,384},{256,0},{384,128},{1,257},{129,385},{257,1},{385... | collective-permute-start | bytes 9224 | tf_op jit(solution)/shard_map/ppermute | solution.py:306
  26.9 2.8 %collective-permute-start.4 = (bf16[2,768]{1,0:T(2,128)(2,1)S(1)}, bf16[2,768]{1,0:T(2,128)(2,1)S(1)}, u32[]{:S(2)}, u32[]{:S(2)}) collective-permute-start(bf16[2,768]{1,0:T(2,128)(2,1)S(1)} %get-tuple-element.14), channel_id=1, source_target_pairs={{0,384},{128,0},{256,128},{384,256},{1,385},{129,1},{257,129},{385... | collective-permute-start | bytes 9224 | tf_op jit(solution)/shard_map/ppermute | solution.py:306
  29.7 2.5 %collective-permute-start.3 = (bf16[2,768]{1,0:T(2,128)(2,1)S(1)}, bf16[2,768]{1,0:T(2,128)(2,1)S(1)}, u32[]{:S(2)}, u32[]{:S(2)}) collective-permute-start(bf16[2,768]{1,0:T(2,128)(2,1)S(1)} %get-tuple-element.14), channel_id=1, source_target_pairs={{0,128},{128,256},{256,384},{384,0},{1,129},{129,257},{257,385},{3... | collective-permute-start | bytes 9224 | tf_op jit(solution)/shard_map/ppermute | solution.py:306
  32.2 0.0 collective-permute-done.5
  32.2 0.0 collective-permute-done.4
  32.3 3.3 %collective-permute-done.3 = bf16[2,768]{1,0:T(2,128)(2,1)S(1)} collective-permute-done((bf16[2,768]{1,0:T(2,128)(2,1)S(1)}, bf16[2,768]{1,0:T(2,128)(2,1)S(1)}, u32[]{:S(2)}, u32[]{:S(2)}) %collective-permute-start.3) | collective-permute-done | bytes 3104 | tf_op jit(solution)/shard_map/ppermute | solution.py:306
  35.6 13.6 %all-to-all-done = bf16[64,2,3840]{2,1,0:T(2,128)(2,1)S(1)} async-done(((bf16[64,2,3840]{2,1,0:T(2,128)(2,1)}), bf16[64,2,3840]{2,1,0:T(2,128)(2,1)S(1)}, u32[]{:S(2)}, u32[]{:S(2)}) %all-to-all-start) | async-done | bytes 983072 | tf_op jit(solution)/shard_map/all_to_all | solution.py:296
  49.2 0.9 broadcast_in_dim.2
  50.2 7.7 %all-to-all-start.1 = ((bf16[64,8,768]{2,1,0:T(8,128)(2,1)}), bf16[64,8,768]{2,1,0:T(8,128)(2,1)S(1)}, u32[]{:S(2)}, u32[]{:S(2)}) async-start(bf16[64,8,768]{2,1,0:T(8,128)(2,1)} %broadcast_in_dim.2), calls=%async_computation.1 | async-start | bytes 1572864 | tf_op jit(solution)/shard_map/all_to_all | solution.py:296
  57.9 0.7 fusion
  58.5 0.2 slice.13.x0
  58.7 3.1 %collective-permute-start = (bf16[64,3840]{1,0:T(8,128)(2,1)S(1)}, bf16[64,3840]{1,0:T(8,128)(2,1)S(1)}, u32[]{:S(2)}, u32[]{:S(2)}) collective-permute-start(bf16[64,3840]{1,0:T(8,128)(2,1)S(1)} %slice.13.x0), channel_id=1, source_target_pairs={{0,128},{128,256},{256,384},{384,0},{1,129},{129,257},{257,385},{3... | collective-permute-start | bytes 1474568 | tf_op jit(solution)/shard_map/ppermute | solution.py:306
  61.9 0.2 slice.15.x1
  62.1 0.0 copy-start
  62.1 3.4 %collective-permute-start.1 = (bf16[64,3840]{1,0:T(8,128)(2,1)S(1)}, bf16[64,3840]{1,0:T(8,128)(2,1)}, u32[]{:S(2)}, u32[]{:S(2)}) collective-permute-start(bf16[64,3840]{1,0:T(8,128)(2,1)S(1)} %slice.15.x1), channel_id=1, source_target_pairs={{0,384},{128,0},{256,128},{384,256},{1,385},{129,1},{257,129},{385... | collective-permute-start | bytes 1474568 | tf_op jit(solution)/shard_map/ppermute | solution.py:306
  65.5 3.2 %collective-permute-start.6 = (bf16[64,3840]{1,0:T(8,128)(2,1)S(1)}, bf16[64,3840]{1,0:T(8,128)(2,1)}, u32[]{:S(2)}, u32[]{:S(2)}) collective-permute-start(bf16[64,3840]{1,0:T(8,128)(2,1)S(1)} %slice.13.x0), channel_id=1, source_target_pairs={{0,384},{128,0},{256,128},{384,256},{1,385},{129,1},{257,129},{385... | collective-permute-start | bytes 1474568 | tf_op jit(solution)/shard_map/ppermute | solution.py:306
  68.6 2.1 %collective-permute-start.7 = (bf16[64,3840]{1,0:T(8,128)(2,1)S(1)}, bf16[64,3840]{1,0:T(8,128)(2,1)}, u32[]{:S(2)}, u32[]{:S(2)}) collective-permute-start(bf16[64,3840]{1,0:T(8,128)(2,1)S(1)} %slice.15.x1), channel_id=1, source_target_pairs={{0,128},{128,256},{256,384},{384,0},{1,129},{129,257},{257,385},{3... | collective-permute-start | bytes 1474568 | tf_op jit(solution)/shard_map/ppermute | solution.py:306
  70.8 2.3 %collective-permute-done.x2 = bf16[64,3840]{1,0:T(8,128)(2,1)S(1)} collective-permute-done((bf16[64,3840]{1,0:T(8,128)(2,1)S(1)}, bf16[64,3840]{1,0:T(8,128)(2,1)S(1)}, u32[]{:S(2)}, u32[]{:S(2)}) %collective-permute-start) | collective-permute-done | bytes 491552 | tf_op jit(solution)/shard_map/ppermute | solution.py:306
  73.1 2.0 %collective-permute-start.8 = (bf16[64,3840]{1,0:T(8,128)(2,1)S(1)}, bf16[64,3840]{1,0:T(8,128)(2,1)}, u32[]{:S(2)}, u32[]{:S(2)}) collective-permute-start(bf16[64,3840]{1,0:T(8,128)(2,1)S(1)} %collective-permute-done.x2), channel_id=1, source_target_pairs={{0,128},{128,256},{256,384},{384,0},{1,129},{129,257},{257,385},{3... | collective-permute-start | bytes 1474568 | tf_op jit(solution)/shard_map/ppermute | solution.py:306
  75.1 0.0 collective-permute-done.1.x3
  75.1 4.5 %collective-permute-start.9 = (bf16[64,3840]{1,0:T(8,128)(2,1)}, bf16[64,3840]{1,0:T(8,128)(2,1)}, u32[]{:S(2)}, u32[]{:S(2)}) collective-permute-start(bf16[64,3840]{1,0:T(8,128)(2,1)} %collective-permute-done.1.x3), channel_id=1, source_target_pairs={{0,384},{128,0},{256,128},{384,256},{1,385},{129,1},{257,129},{385... | collective-permute-start | bytes 1474568 | tf_op jit(solution)/shard_map/ppermute | solution.py:306
  79.6 0.0 collective-permute-done.2.w1
  79.6 0.0 copy-done.1
  79.6 7.4 %early_product.1 = (f32[1024,256]{1,0:T(8,128)S(1)}, f32[16,128]{1,0:T(8,128)S(1)}) custom-call(s32[32]{0:T(128)S(1)} %copy-done.1, bf16[64,3840]{1,0:T(8,128)(2,1)S(1)} %slice.13.x0, bf16[64,3840]{1,0:T(8,128)(2,1)S(1)} %slice.15.x1, bf16[64,3840]{1,0:T(8,128)(2,1)S(1)} %collective-permute-done.x2, bf16[64,3840]{1,0:T(8,128)(2,1)} %collective-permute-done.1.x3, ...), custom_call_target="tpu_custom_call" | custom-call | flops 2013265920 | bytes 10485760 | tf_op jit(solution)/shard_map/early_product/pallas_call | solution.py:146
  87.0 0.0 all-to-all-done.1
  87.1 0.0 copy-done
  87.1 4.0 %mixed_product.1 = (f32[1024,256]{1,0:T(8,128)S(1)}, f32[8,128]{1,0:T(8,128)S(1)}, bf16[1024,3840]{1,0:T(8,128)(2,1)S(1)}) custom-call(s32[8,128]{1,0:T(8,128)S(1)} %bitcast.4, f32[1024,256]{1,0:T(8,128)S(1)} %get-tuple-element.13.near, bf16[512,768]{1,0:T(8,128)(2,1)S(1)} %bitcast.3, bf16[512,4608]{1,0:T(8,128)(2,1)} %w0.3, ...), custom_call_target="tpu_custom_call" | custom-call | flops 805306368 | bytes 12582912 | tf_op jit(solution)/shard_map/mixed_product/pallas_call | solution.py:200
  91.0 0.0 collective-permute-done.6.x0
  91.0 0.0 collective-permute-done.7.x1
  91.1 3.0 %collective-permute-done.8.x2 = bf16[64,3840]{1,0:T(8,128)(2,1)} collective-permute-done((bf16[64,3840]{1,0:T(8,128)(2,1)S(1)}, bf16[64,3840]{1,0:T(8,128)(2,1)}, u32[]{:S(2)}, u32[]{:S(2)}) %collective-permute-start.8) | collective-permute-done | bytes 491552 | tf_op jit(solution)/shard_map/ppermute | solution.py:306
  94.0 2.1 %collective-permute-done.9.x3 = bf16[64,3840]{1,0:T(8,128)(2,1)} collective-permute-done((bf16[64,3840]{1,0:T(8,128)(2,1)}, bf16[64,3840]{1,0:T(8,128)(2,1)}, u32[]{:S(2)}, u32[]{:S(2)}) %collective-permute-start.9) | collective-permute-done | bytes 491552 | tf_op jit(solution)/shard_map/ppermute | solution.py:306
  96.1 3.9 %last_product.1 = f32[32,8,128]{2,1,0:T(8,128)S(1)} custom-call(s32[8,128]{1,0:T(8,128)S(1)} %bitcast.5, f32[1024,256]{1,0:T(8,128)S(1)} %get-tuple-element.15.late, f32[8,128]{1,0:T(8,128)S(1)} %get-tuple-element.16.early_stat, bf16[64,3840]{1,0:T(8,128)(2,1)} %collective-permute-done.6.x0, bf16[64,3840]{1,0:T(8,128)(2,1)} %collective-permute-done.7.x1, ...), custom_call_target="tpu_custom_call" | custom-call | flops 2013265920 | bytes 10485760 | tf_op jit(solution)/shard_map/last_product/pallas_call | solution.py:235
  100.0 17.8 %all_to_all.20.parts = f32[32,8,128]{2,1,0:T(8,128)S(1)} all-to-all(f32[32,8,128]{2,1,0:T(8,128)S(1)} %last_product.1), channel_id=1, replica_groups=mesh['x'=4,'c'=2,'z'=8,'y'=8] {'x','z'}, dimensions={0} | all-to-all | bytes 262144 | tf_op jit(solution)/shard_map/all_to_all | solution.py:296
  117.8 18.0 %all_to_all.21.parts = f32[16,8,128]{2,1,0:T(8,128)S(1)} all-to-all(f32[16,8,128]{2,1,0:T(8,128)S(1)} %join.1), channel_id=1, replica_groups=mesh['x'=4,'c'=2,'z'=8,'y'=8] {'c','y'}, dimensions={0} | all-to-all | bytes 131072 | tf_op jit(solution)/shard_map/all_to_all | solution.py:296
  135.8 0.7 final_loss.1
  (2 shorter events, 0.1 us)
Async XLA Ops:
  0.6 79.0 %copy-start.1 = (s32[32]{0:T(128)S(1)}, s32[32]{0:T(128)}, u32[]{:S(2)}) copy-start(s32[32]{0:T(128)} %lengths.1) | copy-start | bytes 388
  0.6 79.0 %collective-permute-start.2 = (bf16[512,4608]{1,0:T(8,128)(2,1)}, bf16[512,4608]{1,0:T(8,128)(2,1)}, u32[]{:S(2)}, u32[]{:S(2)}) collective-permute-start(bf16[512,4608]{1,0:T(8,128)(2,1)} %w0.3), channel_id=1, source_target_pairs={{0,64},{64,0},{1,65},{65,1},{2,66},{66,2},{3,67},{67,3},{4,68},{68... | collective-permute-start | bytes 14155784 | tf_op jit(solution)/shard_map/ppermute | solution.py:310
  11.3 37.9 %all-to-all-start = ((bf16[64,2,3840]{2,1,0:T(2,128)(2,1)}), bf16[64,2,3840]{2,1,0:T(2,128)(2,1)S(1)}, u32[]{:S(2)}, u32[]{:S(2)}) async-start(bf16[64,2,3840]{2,1,0:T(2,128)(2,1)} %get-tuple-element.11), calls=%async_computation | async-start | bytes 1966080 | tf_op jit(solution)/shard_map/all_to_all | solution.py:296
  22.3 10.0 %collective-permute-start.5 = (bf16[2,768]{1,0:T(2,128)(2,1)S(1)}, bf16[2,768]{1,0:T(2,128)(2,1)S(1)}, u32[]{:S(2)}, u32[]{:S(2)}) collective-permute-start(bf16[2,768]{1,0:T(2,128)(2,1)S(1)} %get-tuple-element.14), channel_id=1, source_target_pairs={{0,256},{128,384},{256,0},{384,128},{1,257},{129,385},{257,1},{385... | collective-permute-start | bytes 9224 | tf_op jit(solution)/shard_map/ppermute | solution.py:306
  26.9 5.3 %collective-permute-start.4 = (bf16[2,768]{1,0:T(2,128)(2,1)S(1)}, bf16[2,768]{1,0:T(2,128)(2,1)S(1)}, u32[]{:S(2)}, u32[]{:S(2)}) collective-permute-start(bf16[2,768]{1,0:T(2,128)(2,1)S(1)} %get-tuple-element.14), channel_id=1, source_target_pairs={{0,384},{128,0},{256,128},{384,256},{1,385},{129,1},{257,129},{385... | collective-permute-start | bytes 9224 | tf_op jit(solution)/shard_map/ppermute | solution.py:306
  29.7 5.8 %collective-permute-start.3 = (bf16[2,768]{1,0:T(2,128)(2,1)S(1)}, bf16[2,768]{1,0:T(2,128)(2,1)S(1)}, u32[]{:S(2)}, u32[]{:S(2)}) collective-permute-start(bf16[2,768]{1,0:T(2,128)(2,1)S(1)} %get-tuple-element.14), channel_id=1, source_target_pairs={{0,128},{128,256},{256,384},{384,0},{1,129},{129,257},{257,385},{3... | collective-permute-start | bytes 9224 | tf_op jit(solution)/shard_map/ppermute | solution.py:306
  50.2 36.9 %all-to-all-start.1 = ((bf16[64,8,768]{2,1,0:T(8,128)(2,1)}), bf16[64,8,768]{2,1,0:T(8,128)(2,1)S(1)}, u32[]{:S(2)}, u32[]{:S(2)}) async-start(bf16[64,8,768]{2,1,0:T(8,128)(2,1)} %broadcast_in_dim.2), calls=%async_computation.1 | async-start | bytes 1572864 | tf_op jit(solution)/shard_map/all_to_all | solution.py:296
  58.7 14.3 %collective-permute-start = (bf16[64,3840]{1,0:T(8,128)(2,1)S(1)}, bf16[64,3840]{1,0:T(8,128)(2,1)S(1)}, u32[]{:S(2)}, u32[]{:S(2)}) collective-permute-start(bf16[64,3840]{1,0:T(8,128)(2,1)S(1)} %slice.13.x0), channel_id=1, source_target_pairs={{0,128},{128,256},{256,384},{384,0},{1,129},{129,257},{257,385},{3... | collective-permute-start | bytes 1474568 | tf_op jit(solution)/shard_map/ppermute | solution.py:306
  62.1 25.0 %copy-start = (s32[1024]{0:T(1024)S(1)}, s32[1024]{0:T(1024)}, u32[]{:S(2)}) copy-start(s32[1024]{0:T(1024)} %param.8) | copy-start | bytes 12292
  62.1 13.0 %collective-permute-start.1 = (bf16[64,3840]{1,0:T(8,128)(2,1)S(1)}, bf16[64,3840]{1,0:T(8,128)(2,1)}, u32[]{:S(2)}, u32[]{:S(2)}) collective-permute-start(bf16[64,3840]{1,0:T(8,128)(2,1)S(1)} %slice.15.x1), channel_id=1, source_target_pairs={{0,384},{128,0},{256,128},{384,256},{1,385},{129,1},{257,129},{385... | collective-permute-start | bytes 1474568 | tf_op jit(solution)/shard_map/ppermute | solution.py:306
  65.5 25.6 %collective-permute-start.6 = (bf16[64,3840]{1,0:T(8,128)(2,1)S(1)}, bf16[64,3840]{1,0:T(8,128)(2,1)}, u32[]{:S(2)}, u32[]{:S(2)}) collective-permute-start(bf16[64,3840]{1,0:T(8,128)(2,1)S(1)} %slice.13.x0), channel_id=1, source_target_pairs={{0,384},{128,0},{256,128},{384,256},{1,385},{129,1},{257,129},{385... | collective-permute-start | bytes 1474568 | tf_op jit(solution)/shard_map/ppermute | solution.py:306
  68.6 22.4 %collective-permute-start.7 = (bf16[64,3840]{1,0:T(8,128)(2,1)S(1)}, bf16[64,3840]{1,0:T(8,128)(2,1)}, u32[]{:S(2)}, u32[]{:S(2)}) collective-permute-start(bf16[64,3840]{1,0:T(8,128)(2,1)S(1)} %slice.15.x1), channel_id=1, source_target_pairs={{0,128},{128,256},{256,384},{384,0},{1,129},{129,257},{257,385},{3... | collective-permute-start | bytes 1474568 | tf_op jit(solution)/shard_map/ppermute | solution.py:306
  73.1 21.0 %collective-permute-start.8 = (bf16[64,3840]{1,0:T(8,128)(2,1)S(1)}, bf16[64,3840]{1,0:T(8,128)(2,1)}, u32[]{:S(2)}, u32[]{:S(2)}) collective-permute-start(bf16[64,3840]{1,0:T(8,128)(2,1)S(1)} %collective-permute-done.x2), channel_id=1, source_target_pairs={{0,128},{128,256},{256,384},{384,0},{1,129},{129,257},{257,385},{3... | collective-permute-start | bytes 1474568 | tf_op jit(solution)/shard_map/ppermute | solution.py:306
  75.1 21.0 %collective-permute-start.9 = (bf16[64,3840]{1,0:T(8,128)(2,1)}, bf16[64,3840]{1,0:T(8,128)(2,1)}, u32[]{:S(2)}, u32[]{:S(2)}) collective-permute-start(bf16[64,3840]{1,0:T(8,128)(2,1)} %collective-permute-done.1.x3), channel_id=1, source_target_pairs={{0,384},{128,0},{256,128},{384,256},{1,385},{129,1},{257,129},{385... | collective-permute-start | bytes 1474568 | tf_op jit(solution)/shard_map/ppermute | solution.py:306
